TPU v7x, 32 devices: a whole 2x2x4 slice. The times are simulated.
32 devices in a mesh: trial: 4 (over x, core), shard: 4 (over z), tp: 2 (over y).
Axes of the slice: x: 2, y: 2, z: 4, core: 2. Of those that a mesh axis runs over, the one named last changes fastest.
Arguments:
- weight_query: bfloat16 [10240, 4096], P(('trial', 'shard'), 'tp'), parts along dimension 0, may hold values from -0.125 to 0.125
- low_query: bfloat16 [10240, 64], P(('trial', 'shard')), parts along dimension 0, may hold values from -0.125 to 0.125
- high_query: bfloat16 [256, 4096], P('trial', 'tp'), parts along dimension 0, may hold values from -0.75 to 0.75
- weight_key: bfloat16 [10240, 1024], P(('trial', 'shard'), 'tp'), parts along dimension 0, may hold values from -0.125 to 0.125
- low_key: bfloat16 [10240, 64], P(('trial', 'shard')), parts along dimension 0, may hold values from -0.125 to 0.125
- high_key: bfloat16 [256, 1024], P('trial', 'tp'), parts along dimension 0, may hold values from -0.75 to 0.75
- weight_value: bfloat16 [10240, 1024], P(('trial', 'shard'), 'tp'), parts along dimension 0, may hold values from -0.125 to 0.125
- low_value: bfloat16 [10240, 64], P(('trial', 'shard')), parts along dimension 0, may hold values from -0.125 to 0.125
- high_value: bfloat16 [256, 1024], P('trial', 'tp'), parts along dimension 0, may hold values from -0.75 to 0.75
- norm_train: float32 [10240], P(('trial', 'shard', 'tp')), parts along dimension 0, may hold values from 0.25 to 1.75
- norm_step: float32 [10240], P(('trial', 'shard', 'tp')), parts along dimension 0, may hold values from -0.3 to 0.3
Outputs:
- serve_query: bfloat16 [16384, 2560], P(('trial', 'tp')), parts along dimension 0
- serve_key: bfloat16 [4096, 2560], P(('trial', 'tp')), parts along dimension 0
- serve_value: bfloat16 [4096, 2560], P(('trial', 'tp')), parts along dimension 0
- serve_norm: bfloat16 [10240], P('trial'), parts along dimension 0
There are 4 independent parts, one for each index of `trial`. A program takes and returns all parts, laid end to end along the dimension named above; each array names one. Nothing has to cross between parts.
All inputs are finite; a program needn't handle non-finite values.
Results may differ from a plain program's by a relative error of at most 0.001.
Values may be sent and summed in bfloat16 or wider, within the bound.
A program may use at most 128 MiB of HBM per device.

v0:
```python
import functools

import jax
import jax.numpy as jnp
from jax import lax
from jax.experimental import pallas as pl
from jax.experimental.pallas import tpu as pltpu
from jax.sharding import PartitionSpec as P

mix_rate = 1.0
MESH = pl.DeviceIdType.MESH
IN_VMEM = True


def chunk_rows(widths):
    for rows in (256, 128):
        if all(width % rows == 0 for width in widths):
            return rows
    return None


def gather_kernel(n, tp, rows, *refs):
    weights, low_refs, high_refs = refs[0:3], refs[3:6], refs[6:9]
    norm_train, norm_step = refs[9:11]
    outs = refs[11:14]
    norm_out = refs[14]
    staged, lows, highs = refs[15], refs[16:19], refs[19:22]
    norm_all, load_sem, small_sem, send_sem, recv_sem, norm_send, norm_recv, norm_ref = refs[22:]
    me, my_tp = lax.axis_index("shard"), lax.axis_index("tp")
    depth = staged.shape[1]
    counts = [weight.shape[1] // rows for weight in weights]
    starts = [sum(counts[:i]) for i in range(len(counts))]
    total = sum(counts)

    def load(which, c):
        return pltpu.make_async_copy(
            weights[which].at[:, pl.ds(pl.multiple_of(c * rows, rows), rows)],
            staged.at[starts[which] + c],
            load_sem.at[starts[which] + c],
        )

    small = [
        (
            pltpu.make_async_copy(low_refs[i], lows[i], small_sem.at[2 * i]),
            pltpu.make_async_copy(high_refs[i], highs[i], small_sem.at[2 * i + 1]),
        )
        for i in range(3)
    ]
    for which in range(3):
        for copy in small[which]:
            copy.start()

        @pl.loop(0, counts[which])
        def _(c):
            load(which, c).start()

    partners = [(k, t) for k in range(n) for t in range(tp) if (k, t) != (0, 0)]

    def partner(k, t):
        return {"shard": lax.rem(me + k, n), "tp": lax.rem(my_tp + t, tp)}

    norm_ref[0, :] = norm_train[...] + norm_step[...]
    barrier = pltpu.get_barrier_semaphore()
    for k, t in partners:
        pl.semaphore_signal(barrier, inc=1, device_id=partner(k, t), device_id_type=MESH)
    pl.semaphore_wait(barrier, len(partners))

    def block(which, c, owner):
        return outs[which].at[
            pl.ds(pl.multiple_of(c * rows, rows), rows),
            pl.ds(pl.multiple_of(owner * depth, 128), depth),
        ]

    def hop(which, c, step, way, owner):
        here = block(which, c, owner)
        slot = ((0 if way > 0 else 1) * (n - 1) + step) * total + starts[which] + c
        return pltpu.make_async_remote_copy(
            here, here, send_sem.at[slot], recv_sem.at[slot],
            device_id={"shard": jnp.clip(me + way, 0, n - 1)}, device_id_type=MESH,
        )

    def sends(step, way):
        owner = me - way * step
        ok = (owner >= 0) & (owner < n) & (me + way >= 0) & (me + way < n)
        return ok, jnp.clip(owner, 0, n - 1)

    def arrives(step, way):
        owner = me - way * (step + 1)
        return (owner >= 0) & (owner < n), jnp.clip(owner, 0, n - 1)

    def send(which, c, step):
        for way in (1, -1):
            ok, owner = sends(step, way)
            pl.when(ok)(lambda: hop(which, c, step, way, owner).start())

    for which in range(3):
        for copy in small[which]:
            copy.wait()

        @pl.loop(0, counts[which])
        def _(c):
            load(which, c).wait()
            high = highs[which][:, pl.ds(pl.multiple_of(c * rows, rows), rows)]
            fresh = staged[starts[which] + c].astype(jnp.float32) + mix_rate * lax.dot_general(
                lows[which][...], high, (((0,), (0,)), ((), ())),
                preferred_element_type=jnp.float32,
            )
            outs[which][
                pl.ds(pl.multiple_of(c * rows, rows), rows),
                pl.ds(pl.multiple_of(me * depth, 128), depth),
            ] = fresh.astype(jnp.bfloat16).T
            send(which, c, 0)

    def norm_copy(i, k, t):
        mine = me * tp + my_tp
        return pltpu.make_async_remote_copy(
            norm_ref, norm_all.at[mine], norm_send.at[i], norm_recv.at[i],
            device_id=partner(k, t), device_id_type=MESH,
        )

    def norm_arrival(i, k, t):
        theirs = lax.rem(me - k + n, n) * tp + lax.rem(my_tp - t + tp, tp)
        return pltpu.make_async_remote_copy(
            norm_ref, norm_all.at[theirs], norm_send.at[i], norm_recv.at[i],
            device_id=partner(k, t), device_id_type=MESH,
        )

    for i, (k, t) in enumerate(partners):
        norm_copy(i, k, t).start()
    norm_all[me * tp + my_tp] = norm_ref[...]

    def pass_on(which, c, step):
        for way in (1, -1):
            ok, owner = arrives(step, way)
            further = ok & (me + way >= 0) & (me + way < n)
            pl.when(ok)(lambda: hop(which, c, step, way, owner).wait_recv())
            if step < n - 2:
                pl.when(further)(lambda: hop(which, c, step + 1, way, owner).start())

    for step in range(n - 1):
        for which in range(3):
            pl.loop(0, counts[which])(functools.partial(pass_on, which, step=step))

        if step == 0:
            for i, (k, t) in enumerate(partners):
                norm_arrival(i, k, t).wait_recv()
            norm_out[...] = norm_all[...].astype(jnp.bfloat16)

    def sent(which, c, step):
        for way in (1, -1):
            ok, owner = sends(step, way)
            pl.when(ok)(lambda: hop(which, c, step, way, owner).wait_send())

    for step in range(n - 1):
        for which in range(3):
            pl.loop(0, counts[which])(functools.partial(sent, which, step=step))

    for i, (k, t) in enumerate(partners):
        norm_copy(i, k, t).wait_send()


def gathered(n, tp, rows, weights, lows, highs, train, step):
    depth = weights[0].shape[0]
    total = sum(weight.shape[1] // rows for weight in weights)
    group, part = n * tp, train.shape[0]
    make = pltpu.VMEM if IN_VMEM else jax.ShapeDtypeStruct
    space = pl.BlockSpec(memory_space=pltpu.VMEM if IN_VMEM else pl.ANY)
    vmem, hbm = pl.BlockSpec(memory_space=pltpu.VMEM), pl.BlockSpec(memory_space=pltpu.HBM)
    return pl.pallas_call(
        functools.partial(gather_kernel, n, tp, rows),
        out_shape=[make((weight.shape[1], n * depth), jnp.bfloat16) for weight in weights]
        + [jax.ShapeDtypeStruct((group, 1, part), jnp.bfloat16)],
        in_specs=[hbm] * 9 + [vmem] * 2,
        out_specs=[space] * 3 + [vmem],
        scratch_shapes=[
            pltpu.VMEM((total, depth, rows), jnp.bfloat16),
            *[pltpu.VMEM(x.shape, x.dtype) for x in (*lows, *highs)],
            pltpu.VMEM((group, 1, part), jnp.float32),
            pltpu.SemaphoreType.DMA((total,)),
            pltpu.SemaphoreType.DMA((6,)),
            pltpu.SemaphoreType.DMA((2 * (n - 1) * total,)),
            pltpu.SemaphoreType.DMA((2 * (n - 1) * total,)),
            pltpu.SemaphoreType.DMA((group - 1,)),
            pltpu.SemaphoreType.DMA((group - 1,)),
            pltpu.VMEM((1, part), jnp.float32),
        ],
        compiler_params=pltpu.CompilerParams(
            collective_id=0, has_side_effects=True, vmem_limit_bytes=47 * 2**20
        ),
    )(*weights, *lows, *highs, train, step)


def flush_kernel(count, *refs):
    sources, results, sems = refs[:count], refs[count : 2 * count], refs[-1]
    copies = [
        pltpu.make_async_copy(source, result, sems.at[i])
        for i, (source, result) in enumerate(zip(sources, results))
    ]
    for copy in copies:
        copy.start()
    for copy in copies:
        copy.wait()


def flushed(held):
    return pl.pallas_call(
        functools.partial(flush_kernel, len(held)),
        out_shape=[jax.ShapeDtypeStruct(x.shape, x.dtype) for x in held],
        in_specs=[pl.BlockSpec(memory_space=pltpu.VMEM)] * len(held),
        out_specs=[pl.BlockSpec(memory_space=pltpu.HBM)] * len(held),
        scratch_shapes=[pltpu.SemaphoreType.DMA((len(held),))],
        compiler_params=pltpu.CompilerParams(vmem_limit_bytes=2**20),
    )(*held)


def plain(weights, lows, highs, norm_new):
    serve = []
    for weight, low, high in zip(weights, lows, highs):
        fresh = weight.astype(jnp.float32) + mix_rate * jnp.dot(
            low, high, preferred_element_type=jnp.float32
        )
        serve.append(
            lax.all_gather(fresh.astype(jnp.bfloat16), "shard", axis=0, tiled=True).T
        )
    norm = lax.all_gather(
        norm_new.astype(jnp.bfloat16), ("shard", "tp"), axis=0, tiled=True
    )
    return (*serve, norm)


def on_device(n, tp, wq, lq, hq, wk, lk, hk, wv, lv, hv, norm_train, norm_step):
    weights, lows, highs = (wq, wk, wv), (lq, lk, lv), (hq, hk, hv)
    rows = chunk_rows([weight.shape[1] for weight in weights])
    if n < 2 or rows is None or wq.shape[0] % 128:
        return plain(weights, lows, highs, norm_train + norm_step)
    *serve, norm = gathered(
        n, tp, rows, weights, [low.T for low in lows], highs, norm_train, norm_step
    )
    return (*flushed(serve), norm.reshape(-1))


def solution(mesh):
    in_specs = (
        (P(("trial", "shard"), "tp"), P(("trial", "shard"), None), P("trial", "tp")) * 3
        + (P(("trial", "shard", "tp")),) * 2
    )
    out_specs = (P(("trial", "tp"), None),) * 3 + (P("trial"),)
    body = functools.partial(on_device, mesh.shape["shard"], mesh.shape["tp"])
    return jax.shard_map(
        body, mesh=mesh, in_specs=in_specs, out_specs=out_specs, check_vma=False
    )
```

profile of v0, /device:TPU:1, one launch (start us, length us, event | category | flops | bytes accessed | tf_op | source)
XLA Modules:
  0.0 269.2 jit_solution(7448410006428014786)
XLA Ops:
  0.6 262.0 %shard_map.138 = (bf16[2048,2560]{1,0:T(8,128)(2,1)S(1)}, bf16[512,2560]{1,0:T(8,128)(2,1)S(1)}, bf16[512,2560]{1,0:T(8,128)(2,1)S(1)}, bf16[8,1,320]{2,1,0:T(2,128)(2,1)}) custom-call(bf16[640,2048]{1,0:T(8,128)(2,1)} %refs_0_.1, bf16[640,512]{1,0:T(8,128)(2,1)} %refs_1_.1, bf16[640,512]{1,0:T(8,128)(2,1)} %refs_2_.1, bf16[64,640]{1,0:T(8,128)(2,1)} %bitcast.3, ...), custom_call_target="tpu_custom_call" | custom-call | tf_op jit(solution)/shard_map/pallas_call | solution.py:169
  262.7 0.0 copy-start
  262.7 5.8 %shard_map.139 = (bf16[2048,2560]{1,0:T(8,128)(2,1)}, bf16[512,2560]{1,0:T(8,128)(2,1)}, bf16[512,2560]{1,0:T(8,128)(2,1)}) custom-call(bf16[2048,2560]{1,0:T(8,128)(2,1)S(1)} %get-tuple-element.11.refs_0_, bf16[512,2560]{1,0:T(8,128)(2,1)S(1)} %get-tuple-element.12.refs_1_, bf16[512,2560]{1,0:T(8,128)(2,1)S(1)} %get-tuple-element.13.refs_2_), custom_call_target="tpu_custom_call" | custom-call | tf_op jit(solution)/shard_map/pallas_call | solution.py:206
  268.5 0.0 copy-done
  268.5 0.7 reshape.11
  (1 shorter events, 0.0 us)
Async XLA Ops:
  262.7 5.8 %copy-start = (bf16[8,1,320]{2,1,0:T(2,128)(2,1)S(1)}, bf16[8,1,320]{2,1,0:T(2,128)(2,1)}, u32[]{:S(2)}) copy-start(bf16[8,1,320]{2,1,0:T(2,128)(2,1)} %get-tuple-element.17) | copy-start | bytes 15364
where the time goes:
time: 271 us; the launch traced here: 269 us
  Pallas kernels  268 us (99%)
    pallas_call x1, Pallas kernels, gathered(): pl.pallas_call(functools.partial(gather_kernel, n, tp, rows), out_shape=[...  262 us
    pallas_call x1, Pallas kernels, flushed(): pl.pallas_call(functools.partial(flush_kernel, len(held)), out_shape=[jax...  5.76 us

commit v1 on v0

v1 whole, which is shorter than its diff:
```python
import functools

import jax
import jax.numpy as jnp
from jax import lax
from jax.experimental import pallas as pl
from jax.experimental.pallas import tpu as pltpu
from jax.sharding import PartitionSpec as P

mix_rate = 1.0
MESH = pl.DeviceIdType.MESH
ROWS = 128
LATE = (4, 1)


def late_from(count):
    first = [max(count - late, 0) for late in LATE]
    core = lax.rem(lax.axis_index("trial"), 2)
    return jnp.where(core == 0, first[0], first[1])


def gather_kernel(n, tp, rows, *refs):
    weights, low_refs, high_refs = refs[0:3], refs[3:6], refs[6:9]
    norm_train, norm_step = refs[9:11]
    outs = refs[11:14]
    norm_out = refs[14]
    staged, lows, highs = refs[15], refs[16:19], refs[19:22]
    (norm_all, load_sem, small_sem, send_sem, recv_sem,
     chain_send, chain_recv, side_send, side_recv, norm_flat) = refs[22:]
    me, my_tp = lax.axis_index("shard"), lax.axis_index("tp")
    depth = staged.shape[1]
    counts = [weight.shape[1] // rows for weight in weights]
    starts = [sum(counts[:i]) for i in range(len(counts))]
    total = sum(counts)
    held_back = late_from(counts[-1])
    last = len(counts) - 1

    def load(which, c):
        return pltpu.make_async_copy(
            weights[which].at[:, pl.ds(pl.multiple_of(c * rows, rows), rows)],
            staged.at[starts[which] + c],
            load_sem.at[starts[which] + c],
        )

    small = [
        (
            pltpu.make_async_copy(low_refs[i], lows[i], small_sem.at[2 * i]),
            pltpu.make_async_copy(high_refs[i], highs[i], small_sem.at[2 * i + 1]),
        )
        for i in range(3)
    ]

    barrier = pltpu.get_barrier_semaphore()
    for way in (1, -1):
        @pl.when((me + way >= 0) & (me + way < n))
        def _():
            pl.semaphore_signal(
                barrier, inc=1, device_id={"shard": jnp.clip(me + way, 0, n - 1)},
                device_id_type=MESH,
            )
    for t in range(1, tp):
        pl.semaphore_signal(
            barrier, inc=1, device_id={"tp": lax.rem(my_tp + t, tp)}, device_id_type=MESH
        )
    for which in range(3):
        for copy in small[which]:
            copy.start()

        @pl.loop(0, counts[which])
        def _(c):
            load(which, c).start()

    def block(which, c, owner):
        return outs[which].at[
            pl.ds(pl.multiple_of(c * rows, rows), rows),
            pl.ds(pl.multiple_of(owner * depth, 128), depth),
        ]

    def lane(step, way):
        return (0 if way > 0 else 1) * (n - 1) + step

    def ahead(way):
        return {"shard": jnp.clip(me + way, 0, n - 1)}

    def hop(which, c, step, way, owner):
        here = block(which, c, owner)
        slot = lane(step, way) * total + starts[which] + c
        return pltpu.make_async_remote_copy(
            here, here, send_sem.at[slot], recv_sem.at[slot],
            device_id=ahead(way), device_id_type=MESH,
        )

    def chain(step, way, owner):
        here = norm_all.at[owner * tp + my_tp]
        return pltpu.make_async_remote_copy(
            here, here, chain_send.at[lane(step, way)], chain_recv.at[lane(step, way)],
            device_id=ahead(way), device_id_type=MESH,
        )

    def side(owner, t, tp_of):
        here = norm_all.at[owner * tp + tp_of]
        slot = owner * (tp - 1) + t - 1
        return pltpu.make_async_remote_copy(
            here, here, side_send.at[slot], side_recv.at[slot],
            device_id={"tp": lax.rem(my_tp + t, tp)}, device_id_type=MESH,
        )

    def end(at, way):
        return at == (n - 1 if way > 0 else 0)

    def sends(step, way):
        owner = me - way * step
        ok = (owner >= 0) & (owner < n) & (me + way >= 0) & (me + way < n)
        return ok, jnp.clip(owner, 0, n - 1)

    def arrives(step, way):
        owner = me - way * (step + 1)
        return (owner >= 0) & (owner < n), jnp.clip(owner, 0, n - 1)

    def now(which, c, at, way):
        if which != last:
            return True
        return (c < held_back) | jnp.logical_not(end(at, way))

    def send(which, c, step):
        for way in (1, -1):
            ok, owner = sends(step, way)
            ok = ok & now(which, c, me + way, way)
            pl.when(ok)(lambda: hop(which, c, step, way, owner).start())

    def merge(which, c):
        load(which, c).wait()
        high = highs[which][:, pl.ds(pl.multiple_of(c * rows, rows), rows)]
        fresh = staged[starts[which] + c].astype(jnp.float32) + mix_rate * lax.dot_general(
            lows[which][...], high, (((0,), (0,)), ((), ())),
            preferred_element_type=jnp.float32,
        )
        outs[which][
            pl.ds(pl.multiple_of(c * rows, rows), rows),
            pl.ds(pl.multiple_of(me * depth, 128), depth),
        ] = fresh.astype(jnp.bfloat16).T

    norm_all[me * tp + my_tp, 0, :] = norm_train[...] + norm_step[...]
    for copy in small[0]:
        copy.wait()
    merge(0, 0)

    inner = jnp.where(me > 0, 1, 0) + jnp.where(me < n - 1, 1, 0)
    pl.semaphore_wait(barrier, inner + tp - 1)
    send(0, 0, 0)
    for way in (1, -1):
        ok, owner = sends(0, way)
        pl.when(ok)(lambda: chain(0, way, owner).start())
    for t in range(1, tp):
        side(me, t, my_tp).start()

    for which in range(3):
        if which:
            for copy in small[which]:
                copy.wait()

        @pl.loop(0 if which else 1, counts[which])
        def _(c):
            merge(which, c)
            send(which, c, 0)

    def pass_norm(step):
        for way in (1, -1):
            ok, owner = arrives(step, way)
            further = ok & (me + way >= 0) & (me + way < n)

            @pl.when(ok)
            def _():
                chain(step, way, owner).wait_recv()
                for t in range(1, tp):
                    side(owner, t, my_tp).start()

            if step < n - 2:
                pl.when(further)(lambda: chain(step + 1, way, owner).start())

    def pass_on(which, c, step):
        for way in (1, -1):
            ok, owner = arrives(step, way)
            further = ok & (me + way >= 0) & (me + way < n) & now(which, c, me + way, way)
            ok = ok & now(which, c, me, way)
            pl.when(ok)(lambda: hop(which, c, step, way, owner).wait_recv())
            if step < n - 2:
                pl.when(further)(lambda: hop(which, c, step + 1, way, owner).start())

    for step in range(n - 1):
        pass_norm(step)
        for which in range(3):
            pl.loop(0, counts[which])(functools.partial(pass_on, which, step=step))

    for owner in range(n):
        for t in range(1, tp):
            side(owner, t, lax.rem(my_tp - t + tp, tp)).wait_recv()
    part = norm_all.shape[2]
    for row in range(norm_out.shape[0]):
        pieces, at = [], row * 128
        while at < (row + 1) * 128:
            slot, lo = divmod(at, part)
            size = min(part - lo, (row + 1) * 128 - at)
            pieces.append(norm_all[slot, 0:1, lo : lo + size])
            at += size
        norm_row = jnp.concatenate(pieces, axis=1) if len(pieces) > 1 else pieces[0]
        norm_flat[row : row + 1, :] = norm_row
    norm_out[...] = norm_flat[...].astype(jnp.bfloat16)

    def sent(which, c, step):
        for way in (1, -1):
            ok, owner = sends(step, way)
            ok = ok & now(which, c, me + way, way)
            pl.when(ok)(lambda: hop(which, c, step, way, owner).wait_send())

    for step in range(n - 1):
        for way in (1, -1):
            ok, owner = sends(step, way)
            pl.when(ok)(lambda: chain(step, way, owner).wait_send())
        for which in range(3):
            pl.loop(0, counts[which])(functools.partial(sent, which, step=step))
    for owner in range(n):
        for t in range(1, tp):
            side(owner, t, my_tp).wait_send()


def gathered(n, tp, rows, weights, lows, highs, train, step):
    depth = weights[0].shape[0]
    total = sum(weight.shape[1] // rows for weight in weights)
    group, part = n * tp, train.shape[0]
    vmem, hbm = pl.BlockSpec(memory_space=pltpu.VMEM), pl.BlockSpec(memory_space=pltpu.HBM)
    return pl.pallas_call(
        functools.partial(gather_kernel, n, tp, rows),
        out_shape=[pltpu.VMEM((weight.shape[1], n * depth), jnp.bfloat16) for weight in weights]
        + [pltpu.VMEM((group * part // 128, 128), jnp.bfloat16)],
        in_specs=[hbm] * 9 + [vmem] * 2,
        out_specs=[vmem] * 4,
        scratch_shapes=[
            pltpu.VMEM((total, depth, rows), jnp.bfloat16),
            *[pltpu.VMEM(x.shape, x.dtype) for x in (*lows, *highs)],
            pltpu.VMEM((group, 1, part), jnp.float32),
            pltpu.SemaphoreType.DMA((total,)),
            pltpu.SemaphoreType.DMA((6,)),
            pltpu.SemaphoreType.DMA((2 * (n - 1) * total,)),
            pltpu.SemaphoreType.DMA((2 * (n - 1) * total,)),
            pltpu.SemaphoreType.DMA((2 * (n - 1),)),
            pltpu.SemaphoreType.DMA((2 * (n - 1),)),
            pltpu.SemaphoreType.DMA((max(n * (tp - 1), 1),)),
            pltpu.SemaphoreType.DMA((max(n * (tp - 1), 1),)),
            pltpu.VMEM((group * part // 128, 128), jnp.float32),
        ],
        compiler_params=pltpu.CompilerParams(
            collective_id=0, has_side_effects=True, vmem_limit_bytes=47 * 2**20
        ),
        name="gather",
    )(*weights, *lows, *highs, train, step)


def flush_kernel(count, *refs):
    sources, results = refs[:count], refs[count : 2 * count]
    token, sems = refs[2 * count :]
    copies = [
        pltpu.make_async_copy(source, result, sems.at[i])
        for i, (source, result) in enumerate(zip(sources, results))
    ]
    for copy in copies:
        copy.start()
    token[...] = jnp.zeros_like(token)
    for copy in copies:
        copy.wait()


def flushed(held):
    return pl.pallas_call(
        functools.partial(flush_kernel, len(held)),
        out_shape=[jax.ShapeDtypeStruct(x.shape, x.dtype) for x in held]
        + [pltpu.VMEM((8, 128), jnp.float32)],
        in_specs=[pl.BlockSpec(memory_space=pltpu.VMEM)] * len(held),
        out_specs=[pl.BlockSpec(memory_space=pltpu.HBM)] * len(held)
        + [pl.BlockSpec(memory_space=pltpu.VMEM)],
        scratch_shapes=[pltpu.SemaphoreType.DMA((len(held),))],
        compiler_params=pltpu.CompilerParams(vmem_limit_bytes=2**20),
        name="flush",
    )(*held)


def tail_kernel(n, rows, depth, held, token, tail, send_sem, recv_sem):
    me = lax.axis_index("shard")
    count = held.shape[0] // rows
    first = late_from(count)
    width = (n - 1) * depth
    ends = ((1, n - 1), (-1, 0))

    barrier = pltpu.get_barrier_semaphore()
    for way, at in ends:
        @pl.when(me == at)
        def _():
            pl.semaphore_signal(
                barrier, inc=1, device_id={"shard": at - way}, device_id_type=MESH
            )

    def copy(c, way, at):
        here = (
            pl.ds(pl.multiple_of(c * rows, rows), rows),
            pl.ds(0 if way > 0 else depth, width),
        )
        slot = (0 if way > 0 else count) + c
        return pltpu.make_async_remote_copy(
            held.at[here], tail.at[here], send_sem.at[slot], recv_sem.at[slot],
            device_id={"shard": at}, device_id_type=MESH,
        )

    greeted = sum(jnp.where(me == at - way, 1, 0) for way, at in ends)
    pl.when(greeted > 0)(lambda: pl.semaphore_wait(barrier, greeted))
    for way, at in ends:
        @pl.when(me == at - way)
        def _():
            pl.loop(first, count)(lambda c: copy(c, way, at).start())
    for way, at in ends:
        @pl.when(me == at)
        def _():
            pl.loop(first, count)(lambda c: copy(c, way, at).wait_recv())
    for way, at in ends:
        @pl.when(me == at - way)
        def _():
            pl.loop(first, count)(lambda c: copy(c, way, at).wait_send())


def tailed(n, rows, depth, held, token):
    vmem = pl.BlockSpec(memory_space=pltpu.VMEM)
    count = held.shape[0] // rows
    return pl.pallas_call(
        functools.partial(tail_kernel, n, rows, depth),
        out_shape=pltpu.VMEM(held.shape, held.dtype),
        in_specs=[vmem, vmem],
        out_specs=vmem,
        scratch_shapes=[
            pltpu.SemaphoreType.DMA((2 * count,)),
            pltpu.SemaphoreType.DMA((2 * count,)),
        ],
        compiler_params=pltpu.CompilerParams(
            collective_id=1, has_side_effects=True, vmem_limit_bytes=2**20
        ),
        name="tail",
    )(held, token)


def close_kernel(n, rows, depth, held, tail, result, sems):
    me = lax.axis_index("shard")
    count = held.shape[0] // rows
    first = late_from(count)
    width = (n - 1) * depth
    outer = (me == 0) | (me == n - 1)

    def whole(c):
        here = pl.ds(pl.multiple_of(c * rows, rows), rows)
        return pltpu.make_async_copy(held.at[here, :], result.at[here, :], sems.at[c])

    def cut(c, at):
        here = pl.ds(pl.multiple_of(c * rows, rows), rows)
        mine = (here, pl.ds(at * depth, depth))
        theirs = (here, pl.ds(0 if at else depth, width))
        return (
            pltpu.make_async_copy(held.at[mine], result.at[mine], sems.at[c]),
            pltpu.make_async_copy(tail.at[theirs], result.at[theirs], sems.at[count + c]),
        )

    bound = jnp.where(outer, first, count)
    pl.loop(0, bound)(lambda c: whole(c).start())
    for at in (0, n - 1):
        @pl.when(me == at)
        def _():
            @pl.loop(first, count)
            def _(c):
                for copy in cut(c, at):
                    copy.start()
    pl.loop(0, bound)(lambda c: whole(c).wait())
    for at in (0, n - 1):
        @pl.when(me == at)
        def _():
            @pl.loop(first, count)
            def _(c):
                for copy in cut(c, at):
                    copy.wait()


def closed(n, rows, depth, held, tail):
    vmem = pl.BlockSpec(memory_space=pltpu.VMEM)
    return pl.pallas_call(
        functools.partial(close_kernel, n, rows, depth),
        out_shape=jax.ShapeDtypeStruct(held.shape, held.dtype),
        in_specs=[vmem, vmem],
        out_specs=pl.BlockSpec(memory_space=pltpu.HBM),
        scratch_shapes=[pltpu.SemaphoreType.DMA((2 * held.shape[0] // rows,))],
        compiler_params=pltpu.CompilerParams(vmem_limit_bytes=2**20),
        name="close",
    )(held, tail)


def plain(weights, lows, highs, norm_new):
    serve = []
    for weight, low, high in zip(weights, lows, highs):
        fresh = weight.astype(jnp.float32) + mix_rate * jnp.dot(
            low, high, preferred_element_type=jnp.float32
        )
        serve.append(
            lax.all_gather(fresh.astype(jnp.bfloat16), "shard", axis=0, tiled=True).T
        )
    norm = lax.all_gather(
        norm_new.astype(jnp.bfloat16), ("shard", "tp"), axis=0, tiled=True
    )
    return (*serve, norm)


def on_device(n, tp, wq, lq, hq, wk, lk, hk, wv, lv, hv, norm_train, norm_step):
    weights, lows, highs = (wq, wk, wv), (lq, lk, lv), (hq, hk, hv)
    depth = wq.shape[0]
    if n < 2 or depth % 128 or any(weight.shape[1] % ROWS for weight in weights):
        return plain(weights, lows, highs, norm_train + norm_step)
    query, key, value, norm = gathered(
        n, tp, ROWS, weights, [low.T for low in lows], highs, norm_train, norm_step
    )
    *done, token = flushed([query, key, norm])
    tail = tailed(n, ROWS, depth, value, token)
    value = closed(n, ROWS, depth, value, tail)
    return (done[0], done[1], value, done[2].reshape(-1))


def solution(mesh):
    in_specs = (
        (P(("trial", "shard"), "tp"), P(("trial", "shard"), None), P("trial", "tp")) * 3
        + (P(("trial", "shard", "tp")),) * 2
    )
    out_specs = (P(("trial", "tp"), None),) * 3 + (P("trial"),)
    body = functools.partial(on_device, mesh.shape["shard"], mesh.shape["tp"])
    return jax.shard_map(
        body, mesh=mesh, in_specs=in_specs, out_specs=out_specs, check_vma=False
    )
```

time: 271 us -> 261 us (0.963)
  Pallas kernels: 268 us -> 258 us
    pallas_call x1, Pallas kernels: 262 us -> 238 us  [gathered(): pl.pallas_call(functools.partial(gather_kernel, n, tp, rows), out_shape=[...]
    pallas_call x0 -> x2, Pallas kernels: none -> 15 us  [the longest x1 13.4 us: tailed(): pl.pallas_call(functools.partial(tail_kernel, n, rows, depth), out_shape=...]
where the time goes in v1:
time: 261 us; the launch traced here: 259 us
  Pallas kernels  258 us (99%)
    pallas_call x1, Pallas kernels, gathered(): pl.pallas_call(functools.partial(gather_kernel, n, tp, rows), out_shape=[...  238 us
    pallas_call x1, Pallas kernels, tailed(): pl.pallas_call(functools.partial(tail_kernel, n, rows, depth), out_shape=...  13.4 us

profile of v1, /device:TPU:1, one launch (start us, length us, event | category | flops | bytes accessed | tf_op | source)
XLA Modules:
  0.0 258.8 jit_solution(480512790257822374)
XLA Ops:
  0.6 238.1 %gather.1 = (bf16[2048,2560]{1,0:T(8,128)(2,1)S(1)}, bf16[512,2560]{1,0:T(8,128)(2,1)S(1)}, bf16[512,2560]{1,0:T(8,128)(2,1)S(1)}, bf16[20,128]{1,0:T(8,128)(2,1)S(1)}) custom-call(bf16[640,2048]{1,0:T(8,128)(2,1)} %refs_0_.1, bf16[640,512]{1,0:T(8,128)(2,1)} %refs_1_.1, bf16[640,512]{1,0:T(8,128)(2,1)} %refs_2_.1, bf16[64,640]{1,0:T(8,128)(2,1)} %bitcast.4, ...), custom_call_target="tpu_custom_call" | custom-call | tf_op jit(solution)/shard_map/gather/pallas_call | solution.py:232
  238.8 5.0 %flush.1 = (bf16[2048,2560]{1,0:T(8,128)(2,1)}, bf16[512,2560]{1,0:T(8,128)(2,1)}, bf16[20,128]{1,0:T(8,128)(2,1)}, f32[8,128]{1,0:T(8,128)S(1)}) custom-call(bf16[2048,2560]{1,0:T(8,128)(2,1)S(1)} %get-tuple-element.12.refs_0_, bf16[512,2560]{1,0:T(8,128)(2,1)S(1)} %get-tuple-element.13.refs_1_, bf16[20,128]{1,0:T(8,128)(2,1)S(1)} %get-tuple-element.14.refs_2_), custom_call_target="tpu_custom_call" | custom-call | tf_op jit(solution)/shard_map/flush/pallas_call | solution.py:274
  243.8 13.4 %tail.1 = bf16[512,2560]{1,0:T(8,128)(2,1)S(1)} custom-call(bf16[512,2560]{1,0:T(8,128)(2,1)S(1)} %get-tuple-element.17.held, f32[8,128]{1,0:T(8,128)S(1)} %get-tuple-element.18.token), custom_call_target="tpu_custom_call" | custom-call | tf_op jit(solution)/shard_map/tail/pallas_call | solution.py:332
  257.2 1.6 close.1

commit v2 on v1

v2 whole, which is shorter than its diff:
```python
import functools

import jax
import jax.numpy as jnp
from jax import lax
from jax.experimental import pallas as pl
from jax.experimental.pallas import tpu as pltpu
from jax.sharding import PartitionSpec as P

mix_rate = 1.0
MESH = pl.DeviceIdType.MESH
ROWS = 128
PIECE = 1024
LATE = (1, 2)


def cut(width, sizes):
    pieces, at = [], 0
    while at < width:
        size = min(sizes[len(pieces)] if len(pieces) < len(sizes) else PIECE, width - at)
        pieces.append((at, size))
        at += size
    return pieces


def last_pieces(width):
    return cut(width, [width - ROWS, ROWS])


def is_late(index, count):
    core = lax.rem(lax.axis_index("trial"), 2)
    late = [index >= count - x for x in LATE]
    if late[0] == late[1]:
        return late[0]
    return core == (0 if late[0] else 1)


def gather_kernel(n, tp, rows, *refs):
    weights, low_refs, high_refs = refs[0:3], refs[3:6], refs[6:9]
    norm_train, norm_step = refs[9:11]
    outs = refs[11:14]
    norm_out = refs[14]
    staged, lows, highs = refs[15], refs[16:19], refs[19:22]
    (norm_all, load_sem, small_sem, send_sem, recv_sem,
     chain_send, chain_recv, side_send, side_recv, norm_flat) = refs[22:]
    me, my_tp = lax.axis_index("shard"), lax.axis_index("tp")
    depth = staged.shape[1]
    counts = [weight.shape[1] // rows for weight in weights]
    starts = [sum(counts[:i]) for i in range(len(counts))]
    total = sum(counts)
    last = len(counts) - 1
    plan = [cut(weight.shape[1], [rows, PIECE - rows] if i == 0 else []) for i, weight in enumerate(weights)]
    plan[last] = last_pieces(weights[last].shape[1])
    pieces = [(which, i, *piece) for which in range(3) for i, piece in enumerate(plan[which])]

    def load(which, c):
        return pltpu.make_async_copy(
            weights[which].at[:, pl.ds(pl.multiple_of(c * rows, rows), rows)],
            staged.at[starts[which] + c],
            load_sem.at[starts[which] + c],
        )

    small = [
        (
            pltpu.make_async_copy(low_refs[i], lows[i], small_sem.at[2 * i]),
            pltpu.make_async_copy(high_refs[i], highs[i], small_sem.at[2 * i + 1]),
        )
        for i in range(3)
    ]

    for copy in small[0]:
        copy.start()
    load(0, 0).start()

    barrier = pltpu.get_barrier_semaphore()
    for way in (1, -1):
        @pl.when((me + way >= 0) & (me + way < n))
        def _():
            pl.semaphore_signal(
                barrier, inc=1, device_id={"shard": jnp.clip(me + way, 0, n - 1)},
                device_id_type=MESH,
            )
    for t in range(1, tp):
        pl.semaphore_signal(
            barrier, inc=1, device_id={"tp": lax.rem(my_tp + t, tp)}, device_id_type=MESH
        )
    for which in range(3):
        if which:
            for copy in small[which]:
                copy.start()

        @pl.loop(0 if which else 1, counts[which])
        def _(c):
            load(which, c).start()

    def block(p, owner):
        which, _, start, size = pieces[p]
        return outs[which].at[
            pl.ds(start, size), pl.ds(pl.multiple_of(owner * depth, 128), depth)
        ]

    def lane(step, way):
        return (0 if way > 0 else 1) * (n - 1) + step

    def ahead(way):
        return {"shard": jnp.clip(me + way, 0, n - 1)}

    def hop(p, step, way, owner):
        here = block(p, owner)
        slot = lane(step, way) * len(pieces) + p
        return pltpu.make_async_remote_copy(
            here, here, send_sem.at[slot], recv_sem.at[slot],
            device_id=ahead(way), device_id_type=MESH,
        )

    def chain(step, way, owner):
        here = norm_all.at[owner * tp + my_tp]
        return pltpu.make_async_remote_copy(
            here, here, chain_send.at[lane(step, way)], chain_recv.at[lane(step, way)],
            device_id=ahead(way), device_id_type=MESH,
        )

    def side(owner, t, tp_of):
        here = norm_all.at[owner * tp + tp_of]
        slot = owner * (tp - 1) + t - 1
        return pltpu.make_async_remote_copy(
            here, here, side_send.at[slot], side_recv.at[slot],
            device_id={"tp": lax.rem(my_tp + t, tp)}, device_id_type=MESH,
        )

    def end(at, way):
        return at == (n - 1 if way > 0 else 0)

    def sends(step, way):
        owner = me - way * step
        ok = (owner >= 0) & (owner < n) & (me + way >= 0) & (me + way < n)
        return ok, jnp.clip(owner, 0, n - 1)

    def arrives(step, way):
        owner = me - way * (step + 1)
        return (owner >= 0) & (owner < n), jnp.clip(owner, 0, n - 1)

    def now(p, at, way):
        which, i = pieces[p][:2]
        if which != last:
            return True
        return jnp.logical_not(is_late(i, len(plan[last])) & end(at, way))

    def send(p, step):
        for way in (1, -1):
            ok, owner = sends(step, way)
            ok = ok & now(p, me + way, way)
            pl.when(ok)(lambda: hop(p, step, way, owner).start())

    def merge(which, c):
        load(which, c).wait()
        high = highs[which][:, pl.ds(pl.multiple_of(c * rows, rows), rows)]
        fresh = staged[starts[which] + c].T.astype(jnp.float32) + mix_rate * lax.dot_general(
            high, lows[which][...], (((0,), (0,)), ((), ())),
            preferred_element_type=jnp.float32,
        )
        outs[which][
            pl.ds(pl.multiple_of(c * rows, rows), rows),
            pl.ds(pl.multiple_of(me * depth, 128), depth),
        ] = fresh.astype(jnp.bfloat16)

    norm_all[me * tp + my_tp, 0, :] = norm_train[...] + norm_step[...]
    for copy in small[0]:
        copy.wait()
    merge(0, 0)

    inner = jnp.where(me > 0, 1, 0) + jnp.where(me < n - 1, 1, 0)
    pl.semaphore_wait(barrier, inner + tp - 1)
    send(0, 0)
    for way in (1, -1):
        ok, owner = sends(0, way)
        pl.when(ok)(lambda: chain(0, way, owner).start())
    for t in range(1, tp):
        side(me, t, my_tp).start()

    for p, (which, i, start, size) in enumerate(pieces):
        if p == 0:
            continue
        if which and i == 0:
            for copy in small[which]:
                copy.wait()
        pl.loop(start // rows, (start + size) // rows)(functools.partial(merge, which))
        send(p, 0)

    def pass_norm(step):
        for way in (1, -1):
            ok, owner = arrives(step, way)
            further = ok & (me + way >= 0) & (me + way < n)

            @pl.when(ok)
            def _():
                chain(step, way, owner).wait_recv()
                for t in range(1, tp):
                    side(owner, t, my_tp).start()

            if step < n - 2:
                pl.when(further)(lambda: chain(step + 1, way, owner).start())

    def pass_on(p, step):
        for way in (1, -1):
            ok, owner = arrives(step, way)
            further = ok & (me + way >= 0) & (me + way < n) & now(p, me + way, way)
            ok = ok & now(p, me, way)
            pl.when(ok)(lambda: hop(p, step, way, owner).wait_recv())
            if step < n - 2:
                pl.when(further)(lambda: hop(p, step + 1, way, owner).start())

    for step in range(n - 1):
        pass_norm(step)
        for p in range(len(pieces)):
            pass_on(p, step)

    for owner in range(n):
        for t in range(1, tp):
            side(owner, t, lax.rem(my_tp - t + tp, tp)).wait_recv()
    part = norm_all.shape[2]
    for row in range(norm_out.shape[0]):
        parts, at = [], row * 128
        while at < (row + 1) * 128:
            slot, lo = divmod(at, part)
            size = min(part - lo, (row + 1) * 128 - at)
            parts.append(norm_all[slot, 0:1, lo : lo + size])
            at += size
        norm_row = jnp.concatenate(parts, axis=1) if len(parts) > 1 else parts[0]
        norm_flat[row : row + 1, :] = norm_row
    norm_out[...] = norm_flat[...].astype(jnp.bfloat16)

    def sent(p, step):
        for way in (1, -1):
            ok, owner = sends(step, way)
            ok = ok & now(p, me + way, way)
            pl.when(ok)(lambda: hop(p, step, way, owner).wait_send())

    for step in range(n - 1):
        for way in (1, -1):
            ok, owner = sends(step, way)
            pl.when(ok)(lambda: chain(step, way, owner).wait_send())
        for p in range(len(pieces)):
            sent(p, step)
    for owner in range(n):
        for t in range(1, tp):
            side(owner, t, my_tp).wait_send()


def gathered(n, tp, rows, weights, lows, highs, train, step):
    depth = weights[0].shape[0]
    total = sum(weight.shape[1] // rows for weight in weights)
    group, part = n * tp, train.shape[0]
    vmem, hbm = pl.BlockSpec(memory_space=pltpu.VMEM), pl.BlockSpec(memory_space=pltpu.HBM)
    return pl.pallas_call(
        functools.partial(gather_kernel, n, tp, rows),
        out_shape=[pltpu.VMEM((weight.shape[1], n * depth), jnp.bfloat16) for weight in weights]
        + [pltpu.VMEM((group * part // 128, 128), jnp.bfloat16)],
        in_specs=[hbm] * 9 + [vmem] * 2,
        out_specs=[vmem] * 4,
        scratch_shapes=[
            pltpu.VMEM((total, depth, rows), jnp.bfloat16),
            *[pltpu.VMEM(x.shape, x.dtype) for x in (*lows, *highs)],
            pltpu.VMEM((group, 1, part), jnp.float32),
            pltpu.SemaphoreType.DMA((total,)),
            pltpu.SemaphoreType.DMA((6,)),
            pltpu.SemaphoreType.DMA((2 * (n - 1) * total,)),
            pltpu.SemaphoreType.DMA((2 * (n - 1) * total,)),
            pltpu.SemaphoreType.DMA((2 * (n - 1),)),
            pltpu.SemaphoreType.DMA((2 * (n - 1),)),
            pltpu.SemaphoreType.DMA((max(n * (tp - 1), 1),)),
            pltpu.SemaphoreType.DMA((max(n * (tp - 1), 1),)),
            pltpu.VMEM((group * part // 128, 128), jnp.float32),
        ],
        compiler_params=pltpu.CompilerParams(
            collective_id=0, has_side_effects=True, vmem_limit_bytes=47 * 2**20
        ),
        name="gather",
    )(*weights, *lows, *highs, train, step)


def flush_kernel(n, count, *refs):
    sources, held = refs[:count], refs[count]
    results, result = refs[count + 1 : 2 * count + 1], refs[2 * count + 1]
    token, sems, held_sems = refs[2 * count + 2 :]
    me = lax.axis_index("shard")
    depth = held.shape[1] // n
    pieces = last_pieces(held.shape[0])
    outer = (me == 0) | (me == n - 1)

    def each(act):
        for i, (source, to) in enumerate(zip(sources, results)):
            act(pltpu.make_async_copy(source, to, sems.at[i]))
        for i, (start, size) in enumerate(pieces):
            rows = pl.ds(start, size)
            late = outer & is_late(i, len(pieces))

            @pl.when(jnp.logical_not(late))
            def _():
                act(pltpu.make_async_copy(
                    held.at[rows, :], result.at[rows, :], held_sems.at[i]
                ))

            @pl.when(late)
            def _():
                here = (rows, pl.ds(pl.multiple_of(me * depth, 128), depth))
                act(pltpu.make_async_copy(held.at[here], result.at[here], held_sems.at[i]))

    each(lambda copy: copy.start())
    token[...] = jnp.zeros_like(token)
    each(lambda copy: copy.wait())


def flushed(n, done, held):
    vmem, hbm = pl.BlockSpec(memory_space=pltpu.VMEM), pl.BlockSpec(memory_space=pltpu.HBM)
    return pl.pallas_call(
        functools.partial(flush_kernel, n, len(done)),
        out_shape=[jax.ShapeDtypeStruct(x.shape, x.dtype) for x in (*done, held)]
        + [pltpu.VMEM((8, 128), jnp.float32)],
        in_specs=[vmem] * (len(done) + 1),
        out_specs=[hbm] * (len(done) + 1) + [vmem],
        scratch_shapes=[
            pltpu.SemaphoreType.DMA((len(done),)),
            pltpu.SemaphoreType.DMA((len(last_pieces(held.shape[0])),)),
        ],
        compiler_params=pltpu.CompilerParams(vmem_limit_bytes=2**20),
        name="flush",
    )(*done, held)


def tail_kernel(n, depth, held, token, tail, send_sem, recv_sem):
    me = lax.axis_index("shard")
    pieces = last_pieces(held.shape[0])
    ends = ((1, n - 1), (-1, 0))

    barrier = pltpu.get_barrier_semaphore()
    for way, at in ends:
        @pl.when(me == at)
        def _():
            pl.semaphore_signal(
                barrier, inc=1, device_id={"shard": at - way}, device_id_type=MESH
            )

    def each(way, at, away, act):
        for i, (start, size) in enumerate(pieces):
            here = (pl.ds(start, size), pl.ds(0 if way > 0 else depth, (n - 1) * depth))
            slot = (0 if way > 0 else len(pieces)) + i

            @pl.when((me == at - away) & is_late(i, len(pieces)))
            def _():
                act(pltpu.make_async_remote_copy(
                    held.at[here], tail.at[here], send_sem.at[slot], recv_sem.at[slot],
                    device_id={"shard": at}, device_id_type=MESH,
                ))

    greeted = sum(jnp.where(me == at - way, 1, 0) for way, at in ends)
    pl.when(greeted > 0)(lambda: pl.semaphore_wait(barrier, greeted))
    for way, at in ends:
        each(way, at, way, lambda copy: copy.start())
    for way, at in ends:
        each(way, at, 0, lambda copy: copy.wait_recv())
    for way, at in ends:
        each(way, at, way, lambda copy: copy.wait_send())


def tailed(n, depth, held, token):
    vmem = pl.BlockSpec(memory_space=pltpu.VMEM)
    count = len(last_pieces(held.shape[0]))
    return pl.pallas_call(
        functools.partial(tail_kernel, n, depth),
        out_shape=pltpu.VMEM(held.shape, held.dtype),
        in_specs=[vmem, vmem],
        out_specs=vmem,
        scratch_shapes=[
            pltpu.SemaphoreType.DMA((2 * count,)),
            pltpu.SemaphoreType.DMA((2 * count,)),
        ],
        compiler_params=pltpu.CompilerParams(
            collective_id=1, has_side_effects=True, vmem_limit_bytes=2**20
        ),
        name="tail",
    )(held, token)


def close_kernel(n, tail, begun, result, sems):
    me = lax.axis_index("shard")
    pieces = last_pieces(tail.shape[0])
    depth = tail.shape[1] // n

    def each(act):
        for at in (0, n - 1):
            for i, (start, size) in enumerate(pieces):
                here = (pl.ds(start, size), pl.ds(0 if at else depth, (n - 1) * depth))

                @pl.when((me == at) & is_late(i, len(pieces)))
                def _():
                    act(pltpu.make_async_copy(tail.at[here], result.at[here], sems.at[i]))

    each(lambda copy: copy.start())
    each(lambda copy: copy.wait())


def closed(n, tail, begun):
    hbm = pl.BlockSpec(memory_space=pltpu.HBM)
    return pl.pallas_call(
        functools.partial(close_kernel, n),
        out_shape=jax.ShapeDtypeStruct(begun.shape, begun.dtype),
        in_specs=[pl.BlockSpec(memory_space=pltpu.VMEM), hbm],
        out_specs=hbm,
        input_output_aliases={1: 0},
        scratch_shapes=[pltpu.SemaphoreType.DMA((len(last_pieces(tail.shape[0])),))],
        compiler_params=pltpu.CompilerParams(vmem_limit_bytes=2**20),
        name="close",
    )(tail, begun)


def plain(weights, lows, highs, norm_new):
    serve = []
    for weight, low, high in zip(weights, lows, highs):
        fresh = weight.astype(jnp.float32) + mix_rate * jnp.dot(
            low, high, preferred_element_type=jnp.float32
        )
        serve.append(
            lax.all_gather(fresh.astype(jnp.bfloat16), "shard", axis=0, tiled=True).T
        )
    norm = lax.all_gather(
        norm_new.astype(jnp.bfloat16), ("shard", "tp"), axis=0, tiled=True
    )
    return (*serve, norm)


def on_device(n, tp, wq, lq, hq, wk, lk, hk, wv, lv, hv, norm_train, norm_step):
    weights, lows, highs = (wq, wk, wv), (lq, lk, lv), (hq, hk, hv)
    depth = wq.shape[0]
    if n < 2 or depth % 128 or any(weight.shape[1] % ROWS for weight in weights) or wv.shape[1] < 2 * ROWS:
        return plain(weights, lows, highs, norm_train + norm_step)
    query, key, value, norm = gathered(
        n, tp, ROWS, weights, [low.T for low in lows], highs, norm_train, norm_step
    )
    *done, begun, token = flushed(n, [query, key, norm], value)
    tail = tailed(n, depth, value, token)
    return (done[0], done[1], closed(n, tail, begun), done[2].reshape(-1))


def solution(mesh):
    in_specs = (
        (P(("trial", "shard"), "tp"), P(("trial", "shard"), None), P("trial", "tp")) * 3
        + (P(("trial", "shard", "tp")),) * 2
    )
    out_specs = (P(("trial", "tp"), None),) * 3 + (P("trial"),)
    body = functools.partial(on_device, mesh.shape["shard"], mesh.shape["tp"])
    return jax.shard_map(
        body, mesh=mesh, in_specs=in_specs, out_specs=out_specs, check_vma=False
    )
```

time: 261 us -> 260 us (level)
    pallas_call x1, Pallas kernels: 238 us -> 218 us  [gathered(): pl.pallas_call(functools.partial(gather_kernel, n, tp, rows), out_shape=[...]
    pallas_call x3, Pallas kernels: 20 us -> 39 us  [the longest x1 32.6 us: tailed(): pl.pallas_call(functools.partial(tail_kernel, n, depth), out_shape=pltpu....]
where the time goes in v2:
time: 260 us; the launch traced here: 258 us
  Pallas kernels  257 us (99%)
    pallas_call x1, Pallas kernels, gathered(): pl.pallas_call(functools.partial(gather_kernel, n, tp, rows), out_shape=[...  218 us
    pallas_call x1, Pallas kernels, tailed(): pl.pallas_call(functools.partial(tail_kernel, n, depth), out_shape=pltpu....  32.6 us

profile of v2, /device:TPU:1, one launch (start us, length us, event | category | flops | bytes accessed | tf_op | source)
XLA Modules:
  0.0 257.8 jit_solution(8956648194684985729)
XLA Ops:
  0.6 218.2 %gather.1 = (bf16[2048,2560]{1,0:T(8,128)(2,1)S(1)}, bf16[512,2560]{1,0:T(8,128)(2,1)S(1)}, bf16[512,2560]{1,0:T(8,128)(2,1)S(1)}, bf16[20,128]{1,0:T(8,128)(2,1)S(1)}) custom-call(bf16[640,2048]{1,0:T(8,128)(2,1)} %refs_0_.1, bf16[640,512]{1,0:T(8,128)(2,1)} %refs_1_.1, bf16[640,512]{1,0:T(8,128)(2,1)} %refs_2_.1, bf16[64,640]{1,0:T(8,128)(2,1)} %bitcast.4, ...), custom_call_target="tpu_custom_call" | custom-call | tf_op jit(solution)/shard_map/gather/pallas_call | solution.py:255
  218.8 5.1 %flush.1 = (bf16[2048,2560]{1,0:T(8,128)(2,1)}, bf16[512,2560]{1,0:T(8,128)(2,1)}, bf16[20,128]{1,0:T(8,128)(2,1)}, bf16[512,2560]{1,0:T(8,128)(2,1)}, f32[8,128]{1,0:T(8,128)S(1)}) custom-call(bf16[2048,2560]{1,0:T(8,128)(2,1)S(1)} %get-tuple-element.13.refs_0_, bf16[512,2560]{1,0:T(8,128)(2,1)S(1)} %get-tuple-element.14.refs_1_, ...), custom_call_target="tpu_custom_call" | custom-call | tf_op jit(solution)/shard_map/flush/pallas_call | solution.py:316
  224.0 32.6 %tail.1 = bf16[512,2560]{1,0:T(8,128)(2,1)S(1)} custom-call(bf16[512,2560]{1,0:T(8,128)(2,1)S(1)} %get-tuple-element.16.refs_3_.held, f32[8,128]{1,0:T(8,128)S(1)} %get-tuple-element.19.token), custom_call_target="tpu_custom_call" | custom-call | tf_op jit(solution)/shard_map/tail/pallas_call | solution.py:369
  256.5 1.3 close.1

commit v3 on v2

--- a/solution.py
+++ b/solution.py
@@ -1,4 +1,5 @@
 import functools
+import math
 
 import jax
 import jax.numpy as jnp
@@ -35,21 +36,20 @@
     return core == (0 if late[0] else 1)
 
 
-def gather_kernel(n, tp, rows, *refs):
+def gather_kernel(n, rows, *refs):
     weights, low_refs, high_refs = refs[0:3], refs[3:6], refs[6:9]
-    norm_train, norm_step = refs[9:11]
-    outs = refs[11:14]
-    norm_out = refs[14]
+    norms = refs[9:11]
+    outs, line = refs[11:14], refs[14]
     staged, lows, highs = refs[15], refs[16:19], refs[19:22]
-    (norm_all, load_sem, small_sem, send_sem, recv_sem,
-     chain_send, chain_recv, side_send, side_recv, norm_flat) = refs[22:]
-    me, my_tp = lax.axis_index("shard"), lax.axis_index("tp")
+    (load_sem, small_sem, send_sem, recv_sem, ready,
+     train, change, norm_sem, chain_send, chain_recv) = refs[22:]
+    me = lax.axis_index("shard")
     depth = staged.shape[1]
     counts = [weight.shape[1] // rows for weight in weights]
     starts = [sum(counts[:i]) for i in range(len(counts))]
     total = sum(counts)
     last = len(counts) - 1
-    plan = [cut(weight.shape[1], [rows, PIECE - rows] if i == 0 else []) for i, weight in enumerate(weights)]
+    plan = [cut(weight.shape[1], [rows, 3 * rows] if i == 0 else []) for i, weight in enumerate(weights)]
     plan[last] = last_pieces(weights[last].shape[1])
     pieces = [(which, i, *piece) for which in range(3) for i, piece in enumerate(plan[which])]
 
@@ -60,38 +60,54 @@
             load_sem.at[starts[which] + c],
         )
 
-    small = [
-        (
-            pltpu.make_async_copy(low_refs[i], lows[i], small_sem.at[2 * i]),
-            pltpu.make_async_copy(high_refs[i], highs[i], small_sem.at[2 * i + 1]),
-        )
-        for i in range(3)
+    def low_copy(which):
+        return pltpu.make_async_copy(low_refs[which], lows[which], small_sem.at[6 + which])
+
+    def high_part(which, part):
+        lo, hi = (0, rows) if part == 0 else (rows, highs[which].shape[1])
+        here = (slice(None), pl.ds(lo, hi - lo))
+        return pltpu.make_async_copy(
+            high_refs[which].at[here], highs[which].at[here], small_sem.at[2 * which + part]
+        )
+
+    load(0, 0).start()
+    low_copy(0).start()
+    high_part(0, 0).start()
+
+    barrier = pltpu.get_barrier_semaphore()
+
+    @pl.when(me < n - 1)
+    def _():
+        pl.semaphore_signal(
+            barrier, inc=1, device_id={"shard": jnp.minimum(me + 1, n - 1)},
+            device_id_type=MESH,
+        )
+
+    @pl.when(me > 0)
+    def _():
+        pl.semaphore_wait(barrier, 1)
+        pl.semaphore_signal(
+            ready, inc=1, device_id={"shard": jnp.maximum(me - 1, 0)}, device_id_type=MESH
+        )
+
+    norm_loads = [
+        pltpu.make_async_copy(norms[0], train, norm_sem.at[0]),
+        pltpu.make_async_copy(norms[1], change, norm_sem.at[1]),
     ]
 
-    for copy in small[0]:
-        copy.start()
-    load(0, 0).start()
-
-    barrier = pltpu.get_barrier_semaphore()
-    for way in (1, -1):
-        @pl.when((me + way >= 0) & (me + way < n))
-        def _():
-            pl.semaphore_signal(
-                barrier, inc=1, device_id={"shard": jnp.clip(me + way, 0, n - 1)},
-                device_id_type=MESH,
-            )
-    for t in range(1, tp):
-        pl.semaphore_signal(
-            barrier, inc=1, device_id={"tp": lax.rem(my_tp + t, tp)}, device_id_type=MESH
-        )
-    for which in range(3):
-        if which:
-            for copy in small[which]:
-                copy.start()
-
-        @pl.loop(0 if which else 1, counts[which])
-        def _(c):
-            load(which, c).start()
+    def load_rest():
+        for copy in norm_loads:
+            copy.start()
+        for which in range(3):
+            if which:
+                low_copy(which).start()
+                high_part(which, 0).start()
+            high_part(which, 1).start()
+
+            @pl.loop(0 if which else 1, counts[which])
+            def _(c):
+                load(which, c).start()
+
 
     def block(p, owner):
         which, _, start, size = pieces[p]
@@ -113,19 +129,11 @@
             device_id=ahead(way), device_id_type=MESH,
         )
 
-    def chain(step, way, owner):
-        here = norm_all.at[owner * tp + my_tp]
+    def chain(hops, way, owner):
+        here = line.at[owner]
         return pltpu.make_async_remote_copy(
-            here, here, chain_send.at[lane(step, way)], chain_recv.at[lane(step, way)],
+            here, here, chain_send.at[lane(hops, way)], chain_recv.at[lane(hops, way)],
             device_id=ahead(way), device_id_type=MESH,
-        )
-
-    def side(owner, t, tp_of):
-        here = norm_all.at[owner * tp + tp_of]
-        slot = owner * (tp - 1) + t - 1
-        return pltpu.make_async_remote_copy(
-            here, here, side_send.at[slot], side_recv.at[slot],
-            device_id={"tp": lax.rem(my_tp + t, tp)}, device_id_type=MESH,
         )
 
     def end(at, way):
@@ -146,11 +154,10 @@
             return True
         return jnp.logical_not(is_late(i, len(plan[last])) & end(at, way))
 
-    def send(p, step):
-        for way in (1, -1):
-            ok, owner = sends(step, way)
-            ok = ok & now(p, me + way, way)
-            pl.when(ok)(lambda: hop(p, step, way, owner).start())
+    def send(p, way):
+        ok, owner = sends(0, way)
+        ok = ok & now(p, me + way, way)
+        pl.when(ok)(lambda: hop(p, 0, way, owner).start())
 
     def merge(which, c):
         load(which, c).wait()
@@ -164,40 +171,37 @@
             pl.ds(pl.multiple_of(me * depth, 128), depth),
         ] = fresh.astype(jnp.bfloat16)
 
-    norm_all[me * tp + my_tp, 0, :] = norm_train[...] + norm_step[...]
-    for copy in small[0]:
+    low_copy(0).wait()
+    high_part(0, 0).wait()
+    merge(0, 0)
+
+    send(0, -1)
+    pl.when(me < n - 1)(lambda: pl.semaphore_wait(ready, 1))
+    send(0, 1)
+    load_rest()
+    for copy in norm_loads:
         copy.wait()
-    merge(0, 0)
-
-    inner = jnp.where(me > 0, 1, 0) + jnp.where(me < n - 1, 1, 0)
-    pl.semaphore_wait(barrier, inner + tp - 1)
-    send(0, 0)
+    line[me, 0, :] = train[...] + change[...]
     for way in (1, -1):
         ok, owner = sends(0, way)
         pl.when(ok)(lambda: chain(0, way, owner).start())
-    for t in range(1, tp):
-        side(me, t, my_tp).start()
-
     for p, (which, i, start, size) in enumerate(pieces):
         if p == 0:
             continue
-        if which and i == 0:
-            for copy in small[which]:
-                copy.wait()
+        if i == 0:
+            low_copy(which).wait()
+            high_part(which, 0).wait()
+        if i == 0 or p == 1:
+            high_part(which, 1).wait()
         pl.loop(start // rows, (start + size) // rows)(functools.partial(merge, which))
-        send(p, 0)
+        send(p, -1)
+        send(p, 1)
 
     def pass_norm(step):
         for way in (1, -1):
             ok, owner = arrives(step, way)
             further = ok & (me + way >= 0) & (me + way < n)
-
-            @pl.when(ok)
-            def _():
-                chain(step, way, owner).wait_recv()
-                for t in range(1, tp):
-                    side(owner, t, my_tp).start()
-
+            pl.when(ok)(lambda: chain(step, way, owner).wait_recv())
             if step < n - 2:
                 pl.when(further)(lambda: chain(step + 1, way, owner).start())
 
@@ -215,21 +219,6 @@
         for p in range(len(pieces)):
             pass_on(p, step)
 
-    for owner in range(n):
-        for t in range(1, tp):
-            side(owner, t, lax.rem(my_tp - t + tp, tp)).wait_recv()
-    part = norm_all.shape[2]
-    for row in range(norm_out.shape[0]):
-        parts, at = [], row * 128
-        while at < (row + 1) * 128:
-            slot, lo = divmod(at, part)
-            size = min(part - lo, (row + 1) * 128 - at)
-            parts.append(norm_all[slot, 0:1, lo : lo + size])
-            at += size
-        norm_row = jnp.concatenate(parts, axis=1) if len(parts) > 1 else parts[0]
-        norm_flat[row : row + 1, :] = norm_row
-    norm_out[...] = norm_flat[...].astype(jnp.bfloat16)
-
     def sent(p, step):
         for way in (1, -1):
             ok, owner = sends(step, way)
@@ -242,35 +231,31 @@
             pl.when(ok)(lambda: chain(step, way, owner).wait_send())
         for p in range(len(pieces)):
             sent(p, step)
-    for owner in range(n):
-        for t in range(1, tp):
-            side(owner, t, my_tp).wait_send()
-
-
-def gathered(n, tp, rows, weights, lows, highs, train, step):
+
+
+def gathered(n, rows, weights, lows, highs, train, step):
     depth = weights[0].shape[0]
     total = sum(weight.shape[1] // rows for weight in weights)
-    group, part = n * tp, train.shape[0]
     vmem, hbm = pl.BlockSpec(memory_space=pltpu.VMEM), pl.BlockSpec(memory_space=pltpu.HBM)
     return pl.pallas_call(
-        functools.partial(gather_kernel, n, tp, rows),
+        functools.partial(gather_kernel, n, rows),
         out_shape=[pltpu.VMEM((weight.shape[1], n * depth), jnp.bfloat16) for weight in weights]
-        + [pltpu.VMEM((group * part // 128, 128), jnp.bfloat16)],
-        in_specs=[hbm] * 9 + [vmem] * 2,
+        + [pltpu.VMEM((n, 1, train.shape[0]), jnp.float32)],
+        in_specs=[hbm] * 11,
         out_specs=[vmem] * 4,
         scratch_shapes=[
             pltpu.VMEM((total, depth, rows), jnp.bfloat16),
             *[pltpu.VMEM(x.shape, x.dtype) for x in (*lows, *highs)],
-            pltpu.VMEM((group, 1, part), jnp.float32),
             pltpu.SemaphoreType.DMA((total,)),
-            pltpu.SemaphoreType.DMA((6,)),
+            pltpu.SemaphoreType.DMA((9,)),
             pltpu.SemaphoreType.DMA((2 * (n - 1) * total,)),
             pltpu.SemaphoreType.DMA((2 * (n - 1) * total,)),
+            pltpu.SemaphoreType.REGULAR,
+            pltpu.VMEM(train.shape, jnp.float32),
+            pltpu.VMEM(step.shape, jnp.float32),
+            pltpu.SemaphoreType.DMA((2,)),
             pltpu.SemaphoreType.DMA((2 * (n - 1),)),
             pltpu.SemaphoreType.DMA((2 * (n - 1),)),
-            pltpu.SemaphoreType.DMA((max(n * (tp - 1), 1),)),
-            pltpu.SemaphoreType.DMA((max(n * (tp - 1), 1),)),
-            pltpu.VMEM((group * part // 128, 128), jnp.float32),
         ],
         compiler_params=pltpu.CompilerParams(
             collective_id=0, has_side_effects=True, vmem_limit_bytes=47 * 2**20
@@ -328,8 +313,21 @@
     )(*done, held)
 
 
-def tail_kernel(n, depth, held, token, tail, send_sem, recv_sem):
-    me = lax.axis_index("shard")
+def lay_out(parts, flat):
+    tp, n, _, part = parts.shape
+    for row in range(flat.shape[0]):
+        cells, at = [], row * 128
+        while at < (row + 1) * 128:
+            slot, lo = divmod(at, part)
+            size = min(part - lo, (row + 1) * 128 - at)
+            cells.append(parts[slot % tp, slot // tp, 0:1, lo : lo + size])
+            at += size
+        flat[row : row + 1, :] = jnp.concatenate(cells, axis=1) if len(cells) > 1 else cells[0]
+
+
+def tail_kernel(n, tp, depth, held, line, token, tail, norm_out, *scratch):
+    lines, norm_flat, send_sem, recv_sem, side_send, side_recv = scratch
+    me, my_tp = lax.axis_index("shard"), lax.axis_index("tp")
     pieces = last_pieces(held.shape[0])
     ends = ((1, n - 1), (-1, 0))
 
@@ -340,6 +338,13 @@
             pl.semaphore_signal(
                 barrier, inc=1, device_id={"shard": at - way}, device_id_type=MESH
             )
+    for t in range(1, tp):
+        pl.semaphore_signal(
+            barrier, inc=1, device_id={"tp": lax.rem(my_tp + t, tp)}, device_id_type=MESH
+        )
+    lines[my_tp] = line[...]
+    greeted = sum(jnp.where(me == at - way, 1, 0) for way, at in ends) + tp - 1
+    pl.when(greeted > 0)(lambda: pl.semaphore_wait(barrier, greeted))
 
     def each(way, at, away, act):
         for i, (start, size) in enumerate(pieces):
@@ -353,36 +358,54 @@
                     device_id={"shard": at}, device_id_type=MESH,
                 ))
 
-    greeted = sum(jnp.where(me == at - way, 1, 0) for way, at in ends)
-    pl.when(greeted > 0)(lambda: pl.semaphore_wait(barrier, greeted))
+    def side(t, column):
+        return pltpu.make_async_remote_copy(
+            line, lines.at[column], side_send.at[t - 1], side_recv.at[t - 1],
+            device_id={"tp": lax.rem(my_tp + t, tp)}, device_id_type=MESH,
+        )
+
     for way, at in ends:
         each(way, at, way, lambda copy: copy.start())
+    for t in range(1, tp):
+        side(t, my_tp).start()
+    for t in range(1, tp):
+        side(t, lax.rem(my_tp - t + tp, tp)).wait_recv()
+    lay_out(lines, norm_flat)
+    norm_out[...] = norm_flat[...].astype(jnp.bfloat16)
     for way, at in ends:
         each(way, at, 0, lambda copy: copy.wait_recv())
     for way, at in ends:
         each(way, at, way, lambda copy: copy.wait_send())
-
-
-def tailed(n, depth, held, token):
+    for t in range(1, tp):
+        side(t, my_tp).wait_send()
+
+
+def tailed(n, tp, depth, held, line, token):
     vmem = pl.BlockSpec(memory_space=pltpu.VMEM)
     count = len(last_pieces(held.shape[0]))
+    lines = (tp, *line.shape)
+    flat = (math.prod(lines) // 128, 128)
     return pl.pallas_call(
-        functools.partial(tail_kernel, n, depth),
-        out_shape=pltpu.VMEM(held.shape, held.dtype),
-        in_specs=[vmem, vmem],
-        out_specs=vmem,
+        functools.partial(tail_kernel, n, tp, depth),
+        out_shape=[pltpu.VMEM(held.shape, held.dtype), pltpu.VMEM(flat, jnp.bfloat16)],
+        in_specs=[vmem] * 3,
+        out_specs=[vmem] * 2,
         scratch_shapes=[
+            pltpu.VMEM(lines, jnp.float32),
+            pltpu.VMEM(flat, jnp.float32),
             pltpu.SemaphoreType.DMA((2 * count,)),
             pltpu.SemaphoreType.DMA((2 * count,)),
+            pltpu.SemaphoreType.DMA((max(tp - 1, 1),)),
+            pltpu.SemaphoreType.DMA((max(tp - 1, 1),)),
         ],
         compiler_params=pltpu.CompilerParams(
             collective_id=1, has_side_effects=True, vmem_limit_bytes=2**20
         ),
         name="tail",
-    )(held, token)
-
-
-def close_kernel(n, tail, begun, result, sems):
+    )(held, line, token)
+
+
+def close_kernel(n, tail, norm, begun, result, norm_out, sems):
     me = lax.axis_index("shard")
     pieces = last_pieces(tail.shape[0])
     depth = tail.shape[1] // n
@@ -395,23 +418,24 @@
                 @pl.when((me == at) & is_late(i, len(pieces)))
                 def _():
                     act(pltpu.make_async_copy(tail.at[here], result.at[here], sems.at[i]))
+        act(pltpu.make_async_copy(norm, norm_out, sems.at[len(pieces)]))
 
     each(lambda copy: copy.start())
     each(lambda copy: copy.wait())
 
 
-def closed(n, tail, begun):
-    hbm = pl.BlockSpec(memory_space=pltpu.HBM)
+def closed(n, tail, norm, begun):
+    vmem, hbm = pl.BlockSpec(memory_space=pltpu.VMEM), pl.BlockSpec(memory_space=pltpu.HBM)
     return pl.pallas_call(
         functools.partial(close_kernel, n),
-        out_shape=jax.ShapeDtypeStruct(begun.shape, begun.dtype),
-        in_specs=[pl.BlockSpec(memory_space=pltpu.VMEM), hbm],
-        out_specs=hbm,
-        input_output_aliases={1: 0},
-        scratch_shapes=[pltpu.SemaphoreType.DMA((len(last_pieces(tail.shape[0])),))],
+        out_shape=[jax.ShapeDtypeStruct(x.shape, x.dtype) for x in (begun, norm)],
+        in_specs=[vmem, vmem, hbm],
+        out_specs=[hbm] * 2,
+        input_output_aliases={2: 0},
+        scratch_shapes=[pltpu.SemaphoreType.DMA((len(last_pieces(tail.shape[0])) + 1,))],
         compiler_params=pltpu.CompilerParams(vmem_limit_bytes=2**20),
         name="close",
-    )(tail, begun)
+    )(tail, norm, begun)
 
 
 def plain(weights, lows, highs, norm_new):
@@ -434,12 +458,13 @@
     depth = wq.shape[0]
     if n < 2 or depth % 128 or any(weight.shape[1] % ROWS for weight in weights) or wv.shape[1] < 2 * ROWS:
         return plain(weights, lows, highs, norm_train + norm_step)
-    query, key, value, norm = gathered(
-        n, tp, ROWS, weights, [low.T for low in lows], highs, norm_train, norm_step
+    query, key, value, line = gathered(
+        n, ROWS, weights, [low.T for low in lows], highs, norm_train, norm_step
     )
-    *done, begun, token = flushed(n, [query, key, norm], value)
-    tail = tailed(n, depth, value, token)
-    return (done[0], done[1], closed(n, tail, begun), done[2].reshape(-1))
+    query, key, begun, token = flushed(n, [query, key], value)
+    tail, norm = tailed(n, tp, depth, value, line, token)
+    value, norm = closed(n, tail, norm, begun)
+    return (query, key, value, norm.reshape(-1))
 
 
 def solution(mesh):

time: 260 us -> 260 us (level)
  no operation moved by 1% of the time
where the time goes in v3:
time: 260 us; the launch traced here: 257 us
  Pallas kernels  257 us (99%)
    pallas_call x1, Pallas kernels, gathered(): pl.pallas_call(functools.partial(gather_kernel, n, rows), out_shape=[pltp...  217 us
    pallas_call x1, Pallas kernels, tailed(): pl.pallas_call(functools.partial(tail_kernel, n, tp, depth), out_shape=[p...  32.7 us

profile of v3, /device:TPU:1, one launch (start us, length us, event | category | flops | bytes accessed | tf_op | source)
XLA Modules:
  0.0 257.3 jit_solution(12810608073378269490)
XLA Ops:
  0.6 217.5 %gather.1 = (bf16[2048,2560]{1,0:T(8,128)(2,1)S(1)}, bf16[512,2560]{1,0:T(8,128)(2,1)S(1)}, bf16[512,2560]{1,0:T(8,128)(2,1)S(1)}, f32[4,1,320]{2,1,0:T(1,128)S(1)}) custom-call(bf16[640,2048]{1,0:T(8,128)(2,1)} %refs_0_.1, bf16[640,512]{1,0:T(8,128)(2,1)} %refs_1_.1, bf16[640,512]{1,0:T(8,128)(2,1)} %refs_2_.1, bf16[64,640]{1,0:T(8,128)(2,1)} %bitcast.4, ...), custom_call_target="tpu_custom_call" | custom-call | tf_op jit(solution)/shard_map/gather/pallas_call | solution.py:240
  218.1 5.2 %flush.1 = (bf16[2048,2560]{1,0:T(8,128)(2,1)}, bf16[512,2560]{1,0:T(8,128)(2,1)}, bf16[512,2560]{1,0:T(8,128)(2,1)}, f32[8,128]{1,0:T(8,128)S(1)}) custom-call(bf16[2048,2560]{1,0:T(8,128)(2,1)S(1)} %get-tuple-element.16.refs_0_, bf16[512,2560]{1,0:T(8,128)(2,1)S(1)} %get-tuple-element.17.refs_1_, bf16[512,2560]{1,0:T(8,128)(2,1)S(1)} %get-tuple-element.18.refs_2_.held), custom_call_target="tpu_custom_call" | custom-call | tf_op jit(solution)/shard_map/flush/pallas_call | solution.py:301
  223.3 32.7 %tail.1 = (bf16[512,2560]{1,0:T(8,128)(2,1)S(1)}, bf16[20,128]{1,0:T(8,128)(2,1)S(1)}) custom-call(bf16[512,2560]{1,0:T(8,128)(2,1)S(1)} %get-tuple-element.18.refs_2_.held, f32[4,1,320]{2,1,0:T(1,128)S(1)} %get-tuple-element.21.line, f32[8,128]{1,0:T(8,128)S(1)} %get-tuple-element.22.token), custom_call_target="tpu_custom_call" | custom-call | tf_op jit(solution)/shard_map/tail/pallas_call | solution.py:388
  256.0 1.3 close.1

commit v4 on v3

--- a/solution.py
+++ b/solution.py
@@ -12,7 +12,8 @@
 MESH = pl.DeviceIdType.MESH
 ROWS = 128
 PIECE = 1024
-LATE = (1, 2)
+LATE = (2, 1)
+YIELD_NS = 4000
 
 
 def cut(width, sizes):
@@ -331,6 +332,9 @@
     pieces = last_pieces(held.shape[0])
     ends = ((1, n - 1), (-1, 0))
 
+    core = lax.rem(lax.axis_index("trial"), 2)
+    pl.when((core == 1) & ((me == 0) | (me == n - 1)))(lambda: pl.delay(YIELD_NS))
+
     barrier = pltpu.get_barrier_semaphore()
     for way, at in ends:
         @pl.when(me == at)

time: 260 us -> 259 us (level)
    pallas_call x1, Pallas kernels: 217 us -> 237 us  [gathered(): pl.pallas_call(functools.partial(gather_kernel, n, rows), out_shape=[pltp...]
    pallas_call x1, Pallas kernels: 32.7 us -> 14.4 us  [tailed(): pl.pallas_call(functools.partial(tail_kernel, n, tp, depth), out_shape=[p...]
where the time goes in v4:
time: 259 us
  Pallas kernels  258 us (100%)
    pallas_call x1, Pallas kernels, gathered(): pl.pallas_call(functools.partial(gather_kernel, n, rows), out_shape=[pltp...  237 us
    pallas_call x1, Pallas kernels, tailed(): pl.pallas_call(functools.partial(tail_kernel, n, tp, depth), out_shape=[p...  14.4 us
    pallas_call x1, Pallas kernels, flushed(): pl.pallas_call(functools.partial(flush_kernel, n, len(done)), out_shape=[...  5.62 us

profile of v4, /device:TPU:1, one launch (start us, length us, event | category | flops | bytes accessed | tf_op | source)
XLA Modules:
  0.0 258.7 jit_solution(5001720998337989037)
XLA Ops:
  0.6 237.3 %gather.1 = (bf16[2048,2560]{1,0:T(8,128)(2,1)S(1)}, bf16[512,2560]{1,0:T(8,128)(2,1)S(1)}, bf16[512,2560]{1,0:T(8,128)(2,1)S(1)}, f32[4,1,320]{2,1,0:T(1,128)S(1)}) custom-call(bf16[640,2048]{1,0:T(8,128)(2,1)} %refs_0_.1, bf16[640,512]{1,0:T(8,128)(2,1)} %refs_1_.1, bf16[640,512]{1,0:T(8,128)(2,1)} %refs_2_.1, bf16[64,640]{1,0:T(8,128)(2,1)} %bitcast.4, ...), custom_call_target="tpu_custom_call" | custom-call | tf_op jit(solution)/shard_map/gather/pallas_call | solution.py:241
  237.9 5.6 %flush.1 = (bf16[2048,2560]{1,0:T(8,128)(2,1)}, bf16[512,2560]{1,0:T(8,128)(2,1)}, bf16[512,2560]{1,0:T(8,128)(2,1)}, f32[8,128]{1,0:T(8,128)S(1)}) custom-call(bf16[2048,2560]{1,0:T(8,128)(2,1)S(1)} %get-tuple-element.16.refs_0_, bf16[512,2560]{1,0:T(8,128)(2,1)S(1)} %get-tuple-element.17.refs_1_, bf16[512,2560]{1,0:T(8,128)(2,1)S(1)} %get-tuple-element.18.refs_2_.held), custom_call_target="tpu_custom_call" | custom-call | tf_op jit(solution)/shard_map/flush/pallas_call | solution.py:302
  243.5 14.4 %tail.1 = (bf16[512,2560]{1,0:T(8,128)(2,1)S(1)}, bf16[20,128]{1,0:T(8,128)(2,1)S(1)}) custom-call(bf16[512,2560]{1,0:T(8,128)(2,1)S(1)} %get-tuple-element.18.refs_2_.held, f32[4,1,320]{2,1,0:T(1,128)S(1)} %get-tuple-element.21.line, f32[8,128]{1,0:T(8,128)S(1)} %get-tuple-element.22.token), custom_call_target="tpu_custom_call" | custom-call | tf_op jit(solution)/shard_map/tail/pallas_call | solution.py:392
  257.9 0.8 close.1

commit v5 on v4

--- a/solution.py
+++ b/solution.py
@@ -50,8 +50,8 @@
     starts = [sum(counts[:i]) for i in range(len(counts))]
     total = sum(counts)
     last = len(counts) - 1
-    plan = [cut(weight.shape[1], [rows, 3 * rows] if i == 0 else []) for i, weight in enumerate(weights)]
-    plan[last] = last_pieces(weights[last].shape[1])
+    widths = [weight.shape[1] for weight in weights]
+    plan = [cut(widths[0], [rows, 3 * rows]), cut(widths[1], []), last_pieces(widths[2])]
     pieces = [(which, i, *piece) for which in range(3) for i, piece in enumerate(plan[which])]
 
     def load(which, c):
@@ -108,7 +108,6 @@
             @pl.loop(0 if which else 1, counts[which])
             def _(c):
                 load(which, c).start()
-
 
     def block(p, owner):
         which, _, start, size = pieces[p]
@@ -460,7 +459,7 @@
 def on_device(n, tp, wq, lq, hq, wk, lk, hk, wv, lv, hv, norm_train, norm_step):
     weights, lows, highs = (wq, wk, wv), (lq, lk, lv), (hq, hk, hv)
     depth = wq.shape[0]
-    if n < 2 or depth % 128 or any(weight.shape[1] % ROWS for weight in weights) or wv.shape[1] < 2 * ROWS:
+    if n < 2 or depth % 128 or any(w.shape[1] % ROWS or w.shape[1] < 2 * ROWS for w in weights):
         return plain(weights, lows, highs, norm_train + norm_step)
     query, key, value, line = gathered(
         n, ROWS, weights, [low.T for low in lows], highs, norm_train, norm_step

time: 259 us -> 259 us (level)
  no operation moved by 1% of the time
where the time goes in v5:
time: 259 us
  Pallas kernels  258 us (100%)
    pallas_call x1, Pallas kernels, gathered(): pl.pallas_call(functools.partial(gather_kernel, n, rows), out_shape=[pltp...  237 us
    pallas_call x1, Pallas kernels, tailed(): pl.pallas_call(functools.partial(tail_kernel, n, tp, depth), out_shape=[p...  14.4 us
    pallas_call x1, Pallas kernels, flushed(): pl.pallas_call(functools.partial(flush_kernel, n, len(done)), out_shape=[...  5.62 us

profile of v5, /device:TPU:1, one launch (start us, length us, event | category | flops | bytes accessed | tf_op | source)
XLA Modules:
  0.0 258.7 jit_solution(5001720998337989037)
XLA Ops:
  0.6 237.3 %gather.1 = (bf16[2048,2560]{1,0:T(8,128)(2,1)S(1)}, bf16[512,2560]{1,0:T(8,128)(2,1)S(1)}, bf16[512,2560]{1,0:T(8,128)(2,1)S(1)}, f32[4,1,320]{2,1,0:T(1,128)S(1)}) custom-call(bf16[640,2048]{1,0:T(8,128)(2,1)} %refs_0_.1, bf16[640,512]{1,0:T(8,128)(2,1)} %refs_1_.1, bf16[640,512]{1,0:T(8,128)(2,1)} %refs_2_.1, bf16[64,640]{1,0:T(8,128)(2,1)} %bitcast.4, ...), custom_call_target="tpu_custom_call" | custom-call | tf_op jit(solution)/shard_map/gather/pallas_call | solution.py:240
  237.9 5.6 %flush.1 = (bf16[2048,2560]{1,0:T(8,128)(2,1)}, bf16[512,2560]{1,0:T(8,128)(2,1)}, bf16[512,2560]{1,0:T(8,128)(2,1)}, f32[8,128]{1,0:T(8,128)S(1)}) custom-call(bf16[2048,2560]{1,0:T(8,128)(2,1)S(1)} %get-tuple-element.16.refs_0_, bf16[512,2560]{1,0:T(8,128)(2,1)S(1)} %get-tuple-element.17.refs_1_, bf16[512,2560]{1,0:T(8,128)(2,1)S(1)} %get-tuple-element.18.refs_2_.held), custom_call_target="tpu_custom_call" | custom-call | tf_op jit(solution)/shard_map/flush/pallas_call | solution.py:301
  243.5 14.4 %tail.1 = (bf16[512,2560]{1,0:T(8,128)(2,1)S(1)}, bf16[20,128]{1,0:T(8,128)(2,1)S(1)}) custom-call(bf16[512,2560]{1,0:T(8,128)(2,1)S(1)} %get-tuple-element.18.refs_2_.held, f32[4,1,320]{2,1,0:T(1,128)S(1)} %get-tuple-element.21.line, f32[8,128]{1,0:T(8,128)S(1)} %get-tuple-element.22.token), custom_call_target="tpu_custom_call" | custom-call | tf_op jit(solution)/shard_map/tail/pallas_call | solution.py:391
  257.9 0.8 close.1

commit v6 on v5

--- a/solution.py
+++ b/solution.py
@@ -11,9 +11,12 @@
 mix_rate = 1.0
 MESH = pl.DeviceIdType.MESH
 ROWS = 128
-PIECE = 1024
+PIECE = 2048
 LATE = (2, 1)
-YIELD_NS = 4000
+YIELD_NS = (2200, 1800)
+SHARE = 8
+AIDED = (1, 0)
+HELPERS = ((3, 0), (1, 1))
 
 
 def cut(width, sizes):
@@ -325,14 +328,43 @@
         flat[row : row + 1, :] = jnp.concatenate(cells, axis=1) if len(cells) > 1 else cells[0]
 
 
-def tail_kernel(n, tp, depth, held, line, token, tail, norm_out, *scratch):
-    lines, norm_flat, send_sem, recv_sem, side_send, side_recv = scratch
+def tail_kernel(n, tp, helpers, depth, held, line, token, tail, norm_out, *scratch):
+    lines, norm_flat, relay, send_sem, recv_sem, side_send, side_recv, aid_send, aid_recv = scratch
+    trial = lax.axis_index("trial")
     me, my_tp = lax.axis_index("shard"), lax.axis_index("tp")
     pieces = last_pieces(held.shape[0])
     ends = ((1, n - 1), (-1, 0))
 
-    core = lax.rem(lax.axis_index("trial"), 2)
-    pl.when((core == 1) & ((me == 0) | (me == n - 1)))(lambda: pl.delay(YIELD_NS))
+    def at_place(place, shard):
+        return (trial == place[0]) & (my_tp == place[1]) & (me == shard)
+
+    def device(place, shard):
+        return {"trial": place[0], "tp": place[1], "shard": shard}
+
+    def legs(h):
+        start = held.shape[0] - (h + 1) * SHARE
+        rows = (pl.ds(start, SHARE), pl.ds(depth, (n - 1) * depth))
+        return (
+            ((AIDED, 1), (helpers[h], 1), held.at[rows], relay),
+            ((helpers[h], 1), (helpers[h], 0), relay, relay),
+            ((helpers[h], 0), (AIDED, 0), relay, tail.at[rows]),
+        )
+
+    def leg(h, k):
+        origin, goal, source, target = legs(h)[k]
+        return origin, goal, pltpu.make_async_remote_copy(
+            source, target, aid_send.at[3 * h + k], aid_recv.at[3 * h + k],
+            device_id=device(*goal), device_id_type=MESH,
+        )
+
+    def start_leg(h, k):
+        origin, _, copy = leg(h, k)
+
+        @pl.when(at_place(*origin))
+        def _():
+            if k:
+                leg(h, k - 1)[2].wait_recv()
+            copy.start()
 
     barrier = pltpu.get_barrier_semaphore()
     for way, at in ends:
@@ -347,19 +379,37 @@
         )
     lines[my_tp] = line[...]
     greeted = sum(jnp.where(me == at - way, 1, 0) for way, at in ends) + tp - 1
+    for h in range(len(helpers)):
+        for k in range(3):
+            origin, goal = legs(h)[k][:2]
+            greeted = greeted + jnp.where(at_place(*origin), 1, 0)
+
+            @pl.when(at_place(*goal))
+            def _():
+                pl.semaphore_signal(
+                    barrier, inc=1, device_id=device(*origin), device_id_type=MESH
+                )
     pl.when(greeted > 0)(lambda: pl.semaphore_wait(barrier, greeted))
 
     def each(way, at, away, act):
         for i, (start, size) in enumerate(pieces):
-            here = (pl.ds(start, size), pl.ds(0 if way > 0 else depth, (n - 1) * depth))
             slot = (0 if way > 0 else len(pieces)) + i
-
-            @pl.when((me == at - away) & is_late(i, len(pieces)))
-            def _():
-                act(pltpu.make_async_remote_copy(
-                    held.at[here], tail.at[here], send_sem.at[slot], recv_sem.at[slot],
-                    device_id={"shard": at}, device_id_type=MESH,
-                ))
+            own = size - len(helpers) * SHARE if i == len(pieces) - 1 else size
+            parts = [(start, own, slot)]
+            if own < size:
+                parts.append((start + own, size - own, 2 * len(pieces) + (0 if way > 0 else 1)))
+            for part, (lo, rows, sem) in enumerate(parts):
+                here = (pl.ds(lo, rows), pl.ds(0 if way > 0 else depth, (n - 1) * depth))
+                ok = (me == at - away) & is_late(i, len(pieces))
+                if part and way < 0:
+                    ok = ok & jnp.logical_not((trial == AIDED[0]) & (my_tp == AIDED[1]))
+
+                @pl.when(ok)
+                def _():
+                    act(pltpu.make_async_remote_copy(
+                        held.at[here], tail.at[here], send_sem.at[sem], recv_sem.at[sem],
+                        device_id={"shard": at}, device_id_type=MESH,
+                    ))
 
     def side(t, column):
         return pltpu.make_async_remote_copy(
@@ -367,12 +417,21 @@
             device_id={"tp": lax.rem(my_tp + t, tp)}, device_id_type=MESH,
         )
 
+    late_core = (lax.rem(trial, 2) == 1) & ((me == 1) | (me == n - 2))
+    for h in range(len(helpers)):
+        start_leg(h, 0)
+    pl.when(late_core)(lambda: pl.delay(YIELD_NS[0]))
+    for h in range(len(helpers)):
+        start_leg(h, 1)
+    pl.when(late_core)(lambda: pl.delay(YIELD_NS[1]))
     for way, at in ends:
         each(way, at, way, lambda copy: copy.start())
     for t in range(1, tp):
         side(t, my_tp).start()
     for t in range(1, tp):
         side(t, lax.rem(my_tp - t + tp, tp)).wait_recv()
+    for h in range(len(helpers)):
+        start_leg(h, 2)
     lay_out(lines, norm_flat)
     norm_out[...] = norm_flat[...].astype(jnp.bfloat16)
     for way, at in ends:
@@ -381,25 +440,33 @@
         each(way, at, way, lambda copy: copy.wait_send())
     for t in range(1, tp):
         side(t, my_tp).wait_send()
-
-
-def tailed(n, tp, depth, held, line, token):
+    for h in range(len(helpers)):
+        pl.when(at_place(AIDED, 0))(lambda: leg(h, 2)[2].wait_recv())
+        for k in range(3):
+            origin, _, copy = leg(h, k)
+            pl.when(at_place(*origin))(copy.wait_send)
+
+
+def tailed(n, tp, helpers, depth, held, line, token):
     vmem = pl.BlockSpec(memory_space=pltpu.VMEM)
     count = len(last_pieces(held.shape[0]))
     lines = (tp, *line.shape)
     flat = (math.prod(lines) // 128, 128)
     return pl.pallas_call(
-        functools.partial(tail_kernel, n, tp, depth),
+        functools.partial(tail_kernel, n, tp, helpers, depth),
         out_shape=[pltpu.VMEM(held.shape, held.dtype), pltpu.VMEM(flat, jnp.bfloat16)],
         in_specs=[vmem] * 3,
         out_specs=[vmem] * 2,
         scratch_shapes=[
             pltpu.VMEM(lines, jnp.float32),
             pltpu.VMEM(flat, jnp.float32),
-            pltpu.SemaphoreType.DMA((2 * count,)),
-            pltpu.SemaphoreType.DMA((2 * count,)),
+            pltpu.VMEM((SHARE, (n - 1) * depth), jnp.bfloat16),
+            pltpu.SemaphoreType.DMA((2 * count + 2,)),
+            pltpu.SemaphoreType.DMA((2 * count + 2,)),
             pltpu.SemaphoreType.DMA((max(tp - 1, 1),)),
             pltpu.SemaphoreType.DMA((max(tp - 1, 1),)),
+            pltpu.SemaphoreType.DMA((max(3 * len(helpers), 1),)),
+            pltpu.SemaphoreType.DMA((max(3 * len(helpers), 1),)),
         ],
         compiler_params=pltpu.CompilerParams(
             collective_id=1, has_side_effects=True, vmem_limit_bytes=2**20
@@ -456,7 +523,7 @@
     return (*serve, norm)
 
 
-def on_device(n, tp, wq, lq, hq, wk, lk, hk, wv, lv, hv, norm_train, norm_step):
+def on_device(trials, n, tp, wq, lq, hq, wk, lk, hk, wv, lv, hv, norm_train, norm_step):
     weights, lows, highs = (wq, wk, wv), (lq, lk, lv), (hq, hk, hv)
     depth = wq.shape[0]
     if n < 2 or depth % 128 or any(w.shape[1] % ROWS or w.shape[1] < 2 * ROWS for w in weights):
@@ -465,7 +532,8 @@
         n, ROWS, weights, [low.T for low in lows], highs, norm_train, norm_step
     )
     query, key, begun, token = flushed(n, [query, key], value)
-    tail, norm = tailed(n, tp, depth, value, line, token)
+    helpers = [place for place in HELPERS if place[0] < trials and place[1] < tp]
+    tail, norm = tailed(n, tp, helpers, depth, value, line, token)
     value, norm = closed(n, tail, norm, begun)
     return (query, key, value, norm.reshape(-1))
 
@@ -476,7 +544,7 @@
         + (P(("trial", "shard", "tp")),) * 2
     )
     out_specs = (P(("trial", "tp"), None),) * 3 + (P("trial"),)
-    body = functools.partial(on_device, mesh.shape["shard"], mesh.shape["tp"])
+    body = functools.partial(on_device, *(mesh.shape[axis] for axis in ("trial", "shard", "tp")))
     return jax.shard_map(
         body, mesh=mesh, in_specs=in_specs, out_specs=out_specs, check_vma=False
     )

time: 259 us -> 259 us (level)
  no operation moved by 1% of the time
where the time goes in v6:
time: 259 us; the launch traced here: 258 us
  Pallas kernels  258 us (100%)
    pallas_call x1, Pallas kernels, gathered(): pl.pallas_call(functools.partial(gather_kernel, n, rows), out_shape=[pltp...  237 us
    pallas_call x1, Pallas kernels, tailed(): pl.pallas_call(functools.partial(tail_kernel, n, tp, helpers, depth), out...  13.8 us
    pallas_call x1, Pallas kernels, flushed(): pl.pallas_call(functools.partial(flush_kernel, n, len(done)), out_shape=[...  5.62 us

profile of v6, /device:TPU:1, one launch (start us, length us, event | category | flops | bytes accessed | tf_op | source)
XLA Modules:
  0.0 258.2 jit_solution(10843490004847647829)
XLA Ops:
  0.6 237.3 %gather.1 = (bf16[2048,2560]{1,0:T(8,128)(2,1)S(1)}, bf16[512,2560]{1,0:T(8,128)(2,1)S(1)}, bf16[512,2560]{1,0:T(8,128)(2,1)S(1)}, f32[4,1,320]{2,1,0:T(1,128)S(1)}) custom-call(bf16[640,2048]{1,0:T(8,128)(2,1)} %refs_0_.1, bf16[640,512]{1,0:T(8,128)(2,1)} %refs_1_.1, bf16[640,512]{1,0:T(8,128)(2,1)} %refs_2_.1, bf16[64,640]{1,0:T(8,128)(2,1)} %bitcast.4, ...), custom_call_target="tpu_custom_call" | custom-call | tf_op jit(solution)/shard_map/gather/pallas_call | solution.py:243
  237.9 5.6 %flush.1 = (bf16[2048,2560]{1,0:T(8,128)(2,1)}, bf16[512,2560]{1,0:T(8,128)(2,1)}, bf16[512,2560]{1,0:T(8,128)(2,1)}, f32[8,128]{1,0:T(8,128)S(1)}) custom-call(bf16[2048,2560]{1,0:T(8,128)(2,1)S(1)} %get-tuple-element.16.refs_0_, bf16[512,2560]{1,0:T(8,128)(2,1)S(1)} %get-tuple-element.17.refs_1_, bf16[512,2560]{1,0:T(8,128)(2,1)S(1)} %get-tuple-element.18.refs_2_.held), custom_call_target="tpu_custom_call" | custom-call | tf_op jit(solution)/shard_map/flush/pallas_call | solution.py:304
  243.5 13.8 %tail.1 = (bf16[512,2560]{1,0:T(8,128)(2,1)S(1)}, bf16[20,128]{1,0:T(8,128)(2,1)S(1)}) custom-call(bf16[512,2560]{1,0:T(8,128)(2,1)S(1)} %get-tuple-element.18.refs_2_.held, f32[4,1,320]{2,1,0:T(1,128)S(1)} %get-tuple-element.21.line, f32[8,128]{1,0:T(8,128)S(1)} %get-tuple-element.22.token), custom_call_target="tpu_custom_call" | custom-call | tf_op jit(solution)/shard_map/tail/pallas_call | solution.py:455
  257.4 0.8 close.1

commit v7 on v5

--- a/solution.py
+++ b/solution.py
@@ -11,9 +11,9 @@
 mix_rate = 1.0
 MESH = pl.DeviceIdType.MESH
 ROWS = 128
-PIECE = 1024
+PIECE = 2048
 LATE = (2, 1)
-YIELD_NS = 4000
+YIELD_NS = 3200
 
 
 def cut(width, sizes):
@@ -26,7 +26,7 @@
 
 
 def last_pieces(width):
-    return cut(width, [width - ROWS, ROWS])
+    return cut(width, [width - ROWS // 2, ROWS // 2])
 
 
 def is_late(index, count):
@@ -193,7 +193,7 @@
             high_part(which, 0).wait()
         if i == 0 or p == 1:
             high_part(which, 1).wait()
-        pl.loop(start // rows, (start + size) // rows)(functools.partial(merge, which))
+        pl.loop(pl.cdiv(start, rows), pl.cdiv(start + size, rows))(functools.partial(merge, which))
         send(p, -1)
         send(p, 1)
 

time: 259 us -> 259 us (level)
    pallas_call x1, Pallas kernels: 14.4 us -> 9.02 us  [tailed(): pl.pallas_call(functools.partial(tail_kernel, n, tp, depth), out_shape=[p...]
    pallas_call x1, Pallas kernels: 237 us -> 243 us  [gathered(): pl.pallas_call(functools.partial(gather_kernel, n, rows), out_shape=[pltp...]
where the time goes in v7:
time: 259 us
  Pallas kernels  258 us (100%)
    pallas_call x1, Pallas kernels, gathered(): pl.pallas_call(functools.partial(gather_kernel, n, rows), out_shape=[pltp...  243 us
    pallas_call x1, Pallas kernels, tailed(): pl.pallas_call(functools.partial(tail_kernel, n, tp, depth), out_shape=[p...  9.02 us
    pallas_call x1, Pallas kernels, flushed(): pl.pallas_call(functools.partial(flush_kernel, n, len(done)), out_shape=[...  5.7 us

profile of v7, /device:TPU:1, one launch (start us, length us, event | category | flops | bytes accessed | tf_op | source)
XLA Modules:
  0.0 258.6 jit_solution(10229977335194414830)
XLA Ops:
  0.6 242.5 %gather.1 = (bf16[2048,2560]{1,0:T(8,128)(2,1)S(1)}, bf16[512,2560]{1,0:T(8,128)(2,1)S(1)}, bf16[512,2560]{1,0:T(8,128)(2,1)S(1)}, f32[4,1,320]{2,1,0:T(1,128)S(1)}) custom-call(bf16[640,2048]{1,0:T(8,128)(2,1)} %refs_0_.1, bf16[640,512]{1,0:T(8,128)(2,1)} %refs_1_.1, bf16[640,512]{1,0:T(8,128)(2,1)} %refs_2_.1, bf16[64,640]{1,0:T(8,128)(2,1)} %bitcast.4, ...), custom_call_target="tpu_custom_call" | custom-call | tf_op jit(solution)/shard_map/gather/pallas_call | solution.py:240
  243.2 5.7 %flush.1 = (bf16[2048,2560]{1,0:T(8,128)(2,1)}, bf16[512,2560]{1,0:T(8,128)(2,1)}, bf16[512,2560]{1,0:T(8,128)(2,1)}, f32[8,128]{1,0:T(8,128)S(1)}) custom-call(bf16[2048,2560]{1,0:T(8,128)(2,1)S(1)} %get-tuple-element.16.refs_0_, bf16[512,2560]{1,0:T(8,128)(2,1)S(1)} %get-tuple-element.17.refs_1_, bf16[512,2560]{1,0:T(8,128)(2,1)S(1)} %get-tuple-element.18.refs_2_.held), custom_call_target="tpu_custom_call" | custom-call | tf_op jit(solution)/shard_map/flush/pallas_call | solution.py:301
  248.9 9.0 %tail.1 = (bf16[512,2560]{1,0:T(8,128)(2,1)S(1)}, bf16[20,128]{1,0:T(8,128)(2,1)S(1)}) custom-call(bf16[512,2560]{1,0:T(8,128)(2,1)S(1)} %get-tuple-element.18.refs_2_.held, f32[4,1,320]{2,1,0:T(1,128)S(1)} %get-tuple-element.21.line, f32[8,128]{1,0:T(8,128)S(1)} %get-tuple-element.22.token), custom_call_target="tpu_custom_call" | custom-call | tf_op jit(solution)/shard_map/tail/pallas_call | solution.py:391
  257.9 0.7 close.1

commit v8 on v5

--- a/solution.py
+++ b/solution.py
@@ -11,7 +11,7 @@
 mix_rate = 1.0
 MESH = pl.DeviceIdType.MESH
 ROWS = 128
-PIECE = 1024
+PIECE = 2048
 LATE = (2, 1)
 YIELD_NS = 4000
 
@@ -71,9 +71,9 @@
             high_refs[which].at[here], highs[which].at[here], small_sem.at[2 * which + part]
         )
 
+    low_copy(0).start(priority=1)
+    high_part(0, 0).start(priority=1)
     load(0, 0).start()
-    low_copy(0).start()
-    high_part(0, 0).start()
 
     barrier = pltpu.get_barrier_semaphore()
 

time: 259 us -> 259 us (level)
  no operation moved by 1% of the time
where the time goes in v8:
time: 259 us
  Pallas kernels  258 us (100%)
    pallas_call x1, Pallas kernels, gathered(): pl.pallas_call(functools.partial(gather_kernel, n, rows), out_shape=[pltp...  237 us
    pallas_call x1, Pallas kernels, tailed(): pl.pallas_call(functools.partial(tail_kernel, n, tp, depth), out_shape=[p...  14.4 us
    pallas_call x1, Pallas kernels, flushed(): pl.pallas_call(functools.partial(flush_kernel, n, len(done)), out_shape=[...  5.62 us

profile of v8, /device:TPU:1, one launch (start us, length us, event | category | flops | bytes accessed | tf_op | source)
XLA Modules:
  0.0 258.7 jit_solution(14419877884812765174)
XLA Ops:
  0.6 237.3 %gather.1 = (bf16[2048,2560]{1,0:T(8,128)(2,1)S(1)}, bf16[512,2560]{1,0:T(8,128)(2,1)S(1)}, bf16[512,2560]{1,0:T(8,128)(2,1)S(1)}, f32[4,1,320]{2,1,0:T(1,128)S(1)}) custom-call(bf16[640,2048]{1,0:T(8,128)(2,1)} %refs_0_.1, bf16[640,512]{1,0:T(8,128)(2,1)} %refs_1_.1, bf16[640,512]{1,0:T(8,128)(2,1)} %refs_2_.1, bf16[64,640]{1,0:T(8,128)(2,1)} %bitcast.4, ...), custom_call_target="tpu_custom_call" | custom-call | tf_op jit(solution)/shard_map/gather/pallas_call | solution.py:240
  237.9 5.6 %flush.1 = (bf16[2048,2560]{1,0:T(8,128)(2,1)}, bf16[512,2560]{1,0:T(8,128)(2,1)}, bf16[512,2560]{1,0:T(8,128)(2,1)}, f32[8,128]{1,0:T(8,128)S(1)}) custom-call(bf16[2048,2560]{1,0:T(8,128)(2,1)S(1)} %get-tuple-element.16.refs_0_, bf16[512,2560]{1,0:T(8,128)(2,1)S(1)} %get-tuple-element.17.refs_1_, bf16[512,2560]{1,0:T(8,128)(2,1)S(1)} %get-tuple-element.18.refs_2_.held), custom_call_target="tpu_custom_call" | custom-call | tf_op jit(solution)/shard_map/flush/pallas_call | solution.py:301
  243.5 14.4 %tail.1 = (bf16[512,2560]{1,0:T(8,128)(2,1)S(1)}, bf16[20,128]{1,0:T(8,128)(2,1)S(1)}) custom-call(bf16[512,2560]{1,0:T(8,128)(2,1)S(1)} %get-tuple-element.18.refs_2_.held, f32[4,1,320]{2,1,0:T(1,128)S(1)} %get-tuple-element.21.line, f32[8,128]{1,0:T(8,128)S(1)} %get-tuple-element.22.token), custom_call_target="tpu_custom_call" | custom-call | tf_op jit(solution)/shard_map/tail/pallas_call | solution.py:391
  257.9 0.8 close.1

commit v9 on v5

--- a/solution.py
+++ b/solution.py
@@ -179,12 +179,15 @@
     pl.when(me < n - 1)(lambda: pl.semaphore_wait(ready, 1))
     send(0, 1)
     load_rest()
-    for copy in norm_loads:
-        copy.wait()
-    line[me, 0, :] = train[...] + change[...]
-    for way in (1, -1):
-        ok, owner = sends(0, way)
-        pl.when(ok)(lambda: chain(0, way, owner).start())
+
+    def start_norm():
+        for copy in norm_loads:
+            copy.wait()
+        line[me, 0, :] = train[...] + change[...]
+        for way in (1, -1):
+            ok, owner = sends(0, way)
+            pl.when(ok)(lambda: chain(0, way, owner).start())
+
     for p, (which, i, start, size) in enumerate(pieces):
         if p == 0:
             continue
@@ -196,6 +199,8 @@
         pl.loop(start // rows, (start + size) // rows)(functools.partial(merge, which))
         send(p, -1)
         send(p, 1)
+        if p == 1:
+            start_norm()
 
     def pass_norm(step):
         for way in (1, -1):

time: 259 us -> 259 us (level)
  no operation moved by 1% of the time
where the time goes in v9:
time: 259 us
  Pallas kernels  258 us (100%)
    pallas_call x1, Pallas kernels, gathered(): pl.pallas_call(functools.partial(gather_kernel, n, rows), out_shape=[pltp...  237 us
    pallas_call x1, Pallas kernels, tailed(): pl.pallas_call(functools.partial(tail_kernel, n, tp, depth), out_shape=[p...  14.4 us
    pallas_call x1, Pallas kernels, flushed(): pl.pallas_call(functools.partial(flush_kernel, n, len(done)), out_shape=[...  5.62 us

profile of v9, /device:TPU:1, one launch (start us, length us, event | category | flops | bytes accessed | tf_op | source)
XLA Modules:
  0.0 258.7 jit_solution(2036005786486877033)
XLA Ops:
  0.6 237.3 %gather.1 = (bf16[2048,2560]{1,0:T(8,128)(2,1)S(1)}, bf16[512,2560]{1,0:T(8,128)(2,1)S(1)}, bf16[512,2560]{1,0:T(8,128)(2,1)S(1)}, f32[4,1,320]{2,1,0:T(1,128)S(1)}) custom-call(bf16[640,2048]{1,0:T(8,128)(2,1)} %refs_0_.1, bf16[640,512]{1,0:T(8,128)(2,1)} %refs_1_.1, bf16[640,512]{1,0:T(8,128)(2,1)} %refs_2_.1, bf16[64,640]{1,0:T(8,128)(2,1)} %bitcast.4, ...), custom_call_target="tpu_custom_call" | custom-call | tf_op jit(solution)/shard_map/gather/pallas_call | solution.py:245
  237.9 5.6 %flush.1 = (bf16[2048,2560]{1,0:T(8,128)(2,1)}, bf16[512,2560]{1,0:T(8,128)(2,1)}, bf16[512,2560]{1,0:T(8,128)(2,1)}, f32[8,128]{1,0:T(8,128)S(1)}) custom-call(bf16[2048,2560]{1,0:T(8,128)(2,1)S(1)} %get-tuple-element.16.refs_0_, bf16[512,2560]{1,0:T(8,128)(2,1)S(1)} %get-tuple-element.17.refs_1_, bf16[512,2560]{1,0:T(8,128)(2,1)S(1)} %get-tuple-element.18.refs_2_.held), custom_call_target="tpu_custom_call" | custom-call | tf_op jit(solution)/shard_map/flush/pallas_call | solution.py:306
  243.5 14.4 %tail.1 = (bf16[512,2560]{1,0:T(8,128)(2,1)S(1)}, bf16[20,128]{1,0:T(8,128)(2,1)S(1)}) custom-call(bf16[512,2560]{1,0:T(8,128)(2,1)S(1)} %get-tuple-element.18.refs_2_.held, f32[4,1,320]{2,1,0:T(1,128)S(1)} %get-tuple-element.21.line, f32[8,128]{1,0:T(8,128)S(1)} %get-tuple-element.22.token), custom_call_target="tpu_custom_call" | custom-call | tf_op jit(solution)/shard_map/tail/pallas_call | solution.py:396
  257.9 0.8 close.1
